TPU v7x, 32 devices: a whole 2x2x4 slice. The times are simulated.
32 devices in a mesh: band: 16 (over z, y, core), ga: 2 (over x).
Axes of the slice: x: 2, y: 2, z: 4, core: 2. Of those that a mesh axis runs over, the one named last changes fastest.
Arguments:
- orbitals: bfloat16 [2, 16, 160, 128], P(None, 'band', 'ga'), may hold values from -8 to 8, as said below
- potential: float32 [480, 480], P('ga'), may hold values from -2 to 2
- slot_sticks: int32 [160], replicated, may hold values from -1 to 126, as said below
- stick_entries: int32 [160, 128], replicated, may hold values from -1 to 126, as said below
Outputs:
- applied_orbitals: bfloat16 [2, 16, 160, 128], P(None, 'band', 'ga')
- correlation: float32 [2, 16, 16], replicated
- reduced_hamiltonian: float32 [2, 16, 16], replicated
Inputs may be any that keep to these rules, and one draw needn't show every extreme that they name: `slot_sticks`: every gx with |gx| < 64 is held by exactly one slot; the other slots hold -1. Slots t with t // 80 = d are those of index d of ga; on some index of ga all 80 slots hold sticks. `stick_entries`: row t lists, in some order, gz + 63 for every gz with gx^2 + gz^2 < 64^2, gx being the stick of slot t, then -1 to the end of the row; rows of empty slots are all -1. `orbitals`: entries where stick_entries is -1 carry values that are not used.
All inputs are finite; a program needn't handle non-finite values.
Results may differ from a plain program's by a relative error of at most 0.001.
Values may be sent and summed in bfloat16 or wider, within the bound.
A program may use at most 64 MiB of HBM per device.

v0:
```python
import functools

import jax
import jax.numpy as jnp
import numpy as np
from jax import lax
from jax.experimental import pallas as pl
from jax.experimental.pallas import tpu as pltpu
from jax.sharding import PartitionSpec as P

MESH = pl.DeviceIdType.MESH
NT = (((1,), (1,)), ((), ()))
BF16 = jnp.bfloat16
F32 = jnp.float32


def split_np(table):
    high = table.astype(np.float32).astype(BF16)
    low = (table - high.astype(np.float64)).astype(np.float32).astype(BF16)
    return np.stack([high, low])


def tables(points, width, radius, groups, planes, plane_pad, coarse):
    freq = np.arange(width) - radius + 1
    used = (np.arange(width) < width - 1).astype(np.float64)
    z_tabs = []
    for group in range(groups):
        z = np.arange(planes) + group * planes
        angle = 2.0 * np.pi * ((freq[:, None] * z[None, :]) % points) / points
        cos = np.zeros((width, plane_pad))
        sin = np.zeros((width, plane_pad))
        cos[:, :planes] = np.cos(angle) * used[:, None]
        sin[:, :planes] = np.sin(angle) * used[:, None]
        z_tabs.append(split_np(np.block([[cos, sin], [-sin, cos]])))
    x = np.arange(coarse)
    angle = 2.0 * np.pi * ((freq[None, :] * x[:, None]) % coarse) / coarse
    cos = np.cos(angle) * used[None, :]
    sin = np.sin(angle) * used[None, :]
    forward = np.block([[cos, -sin], [sin, cos]])
    limit = 2 * (radius - 1)
    offset = (x[:, None] * points - np.arange(points)[None, :] * coarse) % (coarse * points)
    base = 2.0 * np.pi * offset / (coarse * points)
    resample = np.ones((coarse, points))
    for g in range(1, limit + 1):
        resample += 2.0 * np.cos(g * base)
    resample /= points
    return (
        np.stack(z_tabs),
        split_np(forward),
        split_np(forward.T.copy()),
        split_np(resample),
    )


def split(value):
    high = value.astype(BF16)
    low = (value - high.astype(F32)).astype(BF16)
    return high, low


def dot(a, b):
    return jnp.dot(a, b, preferred_element_type=F32)


def dot_nt(a, b):
    return lax.dot_general(a, b, NT, preferred_element_type=F32)


def take_lanes(value, index):
    return jnp.take_along_axis(value, index, axis=1, mode="promise_in_bounds")


def kernel(
    bands,
    groups,
    points,
    radius,
    orb_hbm,
    slots_hbm,
    entries_hbm,
    pot_hbm,
    tz_hbm,
    tx_hbm,
    ty_hbm,
    tr_hbm,
    out_ref,
    corr_ref,
    red_ref,
    orb_ref,
    slots_ref,
    entries_ref,
    tz,
    tx,
    ty,
    tr,
    pot,
    spread,
    colbuf,
    part,
    got,
    gather,
    sums,
    message,
    inbox,
    load_sem,
    s_send,
    s_recv,
    p_send,
    p_recv,
    g_send,
    g_recv,
    m_send,
    m_recv,
):
    band = lax.axis_index("band")
    ga = lax.axis_index("ga")
    total = bands * groups
    half = bands // 2
    me = ga * bands + band
    slots = orb_hbm.shape[2]
    width = orb_hbm.shape[3]
    planes = pot_hbm.shape[0]
    plane_pad = pot.shape[0]
    coarse = ty.shape[2] // 2
    msg_width = message.shape[1]

    def where_is(index):
        return (lax.rem(index, bands), lax.div(index, bands))

    barrier = pltpu.get_barrier_semaphore()

    @pl.loop(1, total)
    def _(k):
        pl.semaphore_signal(
            barrier, inc=1, device_id=where_is(lax.rem(me + k, total)), device_id_type=MESH
        )

    first = [
        pltpu.make_async_copy(
            entries_hbm.at[pl.ds(pl.multiple_of(ga * slots, 8), slots)], entries_ref, load_sem.at[5]
        ),
        pltpu.make_async_copy(orb_hbm, orb_ref, load_sem.at[6]),
        pltpu.make_async_copy(slots_hbm, slots_ref, load_sem.at[7]),
    ]
    for load in first:
        load.start()
    loads = [
        pltpu.make_async_copy(pot_hbm, pot.at[pl.ds(0, planes)], load_sem.at[0]),
        pltpu.make_async_copy(tr_hbm, tr, load_sem.at[1]),
        pltpu.make_async_copy(tz_hbm.at[ga], tz, load_sem.at[2]),
        pltpu.make_async_copy(tx_hbm, tx, load_sem.at[3]),
        pltpu.make_async_copy(ty_hbm, ty, load_sem.at[4]),
    ]
    for load in loads:
        load.start()
    if plane_pad > planes:
        pot[pl.ds(planes, plane_pad - planes), :] = jnp.zeros(
            (plane_pad - planes, pot.shape[1]), F32
        )

    sums[...] = jnp.zeros_like(sums)

    for load in first:
        load.wait()
    own = entries_ref[...]
    all_sticks = slots_ref[...].reshape(1, groups * slots)
    sticks = [all_sticks[:, g * slots : (g + 1) * slots] for g in range(groups)]
    lane = lax.broadcasted_iota(jnp.int32, (slots, width), 1)
    inverse = jnp.full((slots, width), -1, jnp.int32)
    for k in range(width):
        inverse = jnp.where(own[:, k : k + 1] == lane, k, inverse)
    re = orb_ref[0, 0].astype(F32)
    im = orb_ref[1, 0].astype(F32)
    filled = inverse >= 0
    index = jnp.maximum(inverse, 0)
    spread[ga, :, :width] = jnp.where(filled, take_lanes(re, index), 0.0).astype(BF16)
    spread[ga, :, width:] = jnp.where(filled, take_lanes(im, index), 0.0).astype(BF16)

    pl.semaphore_wait(barrier, total - 1)

    s_copies = []
    for k in range(1, groups):
        copy = pltpu.make_async_remote_copy(
            src_ref=spread.at[ga],
            dst_ref=spread.at[ga],
            send_sem=s_send.at[k - 1],
            recv_sem=s_recv.at[k - 1],
            device_id=(band, lax.rem(ga + k, groups)),
            device_id_type=MESH,
        )
        copy.start()
        s_copies.append(copy)

    def gather_copy(k):
        return pltpu.make_async_remote_copy(
            src_ref=orb_hbm.at[:, 0],
            dst_ref=gather.at[k],
            send_sem=g_send.at[k],
            recv_sem=g_recv.at[k],
            device_id=(lax.rem(band + k, bands), ga),
            device_id_type=MESH,
        )

    @pl.loop(1, half + 1)
    def _(k):
        gather_copy(k).start()

    loads[0].wait()
    loads[1].wait()
    pot_hi, pot_lo = split(pot[...])
    weight = dot_nt(tr[0], pot_hi) + dot_nt(tr[0], pot_lo) + dot_nt(tr[1], pot_hi)

    for copy in s_copies:
        copy.wait()
    dense = jnp.zeros((width, 2 * width), F32)
    sub = lax.broadcasted_iota(jnp.int32, (width, slots), 0)
    for g in range(groups):
        choose = jnp.where(sub == sticks[g], 1.0, 0.0).astype(BF16)
        dense += dot(choose, spread[g])
    dense = dense.astype(BF16)

    loads[2].wait()
    columns = dot(dense, tz[0]) + dot(dense, tz[1])
    col_hi, col_lo = split(columns)
    colbuf[0, :width] = col_hi[:, :plane_pad]
    colbuf[0, width:] = col_hi[:, plane_pad:]
    colbuf[1, :width] = col_lo[:, :plane_pad]
    colbuf[1, width:] = col_lo[:, plane_pad:]
    loads[3].wait()
    field = dot(tx[0], colbuf[0]) + dot(tx[0], colbuf[1]) + dot(tx[1], colbuf[0])
    product = jnp.concatenate([field[:coarse] * weight, field[coarse:] * weight], axis=0)
    pro_hi, pro_lo = split(product)
    loads[4].wait()
    back = dot(ty[0], pro_hi) + dot(ty[0], pro_lo) + dot(ty[1], pro_hi)
    back = jnp.concatenate([back[:width], back[width:]], axis=1)
    back_hi, back_lo = split(back)
    spectra = dot_nt(back_hi, tz[0]) + dot_nt(back_hi, tz[1]) + dot_nt(back_lo, tz[0])
    spectra = spectra * (1.0 / float(points * coarse))
    spec_hi, spec_lo = split(spectra)

    eye = lax.broadcasted_iota(jnp.int32, (slots, slots), 0) == lax.broadcasted_iota(
        jnp.int32, (slots, slots), 1
    )

    def stick_column(g):
        row = sticks[0]
        for other in range(1, groups):
            row = jnp.where(g == other, sticks[other], row)
        row = row.astype(F32)
        return jnp.sum(jnp.where(eye, row, 0.0), axis=1, keepdims=True)

    lane_f = lane.astype(F32)
    p_copies = []
    for k in range(1, groups + 1):
        target = lax.rem(ga + k, groups)
        stick = stick_column(target)
        choose = jnp.where(stick == lane_f, 1.0, 0.0).astype(BF16)
        mine = dot(choose, spec_hi) + dot(choose, spec_lo)
        if k < groups:
            part[k - 1] = mine
            copy = pltpu.make_async_remote_copy(
                src_ref=part.at[k - 1],
                dst_ref=got.at[k - 1],
                send_sem=p_send.at[k - 1],
                recv_sem=p_recv.at[k - 1],
                device_id=(band, target),
                device_id_type=MESH,
            )
            copy.start()
            p_copies.append(copy)

    present = own >= 0
    gx = stick - float(radius - 1)
    gz = (own - (radius - 1)).astype(F32)
    kinetic = (gx * gx + gz * gz) * (1.0 / float(radius * radius))
    own_index = jnp.maximum(own, 0)

    gather[0] = orb_ref[:, 0]
    m_re = jnp.where(present, re, 0.0)
    m_im = jnp.where(present, im, 0.0)

    def add_products(first, right_re, right_im, fresh):
        @pl.loop(0, half + 1)
        def _(k):
            if fresh:
                @pl.when(k > 0)
                def _():
                    gather_copy(k).wait()

            b = lax.rem(band - k + bands, bands)
            left_re = gather[k, 0].astype(F32)
            left_im = gather[k, 1].astype(F32)
            real = left_re * right_re + left_im * right_im
            imag = left_re * right_im - left_im * right_re
            sums[pl.ds(first * bands + b, 1), :] = jnp.sum(real, axis=0, keepdims=True)
            sums[pl.ds((first + 1) * bands + b, 1), :] = jnp.sum(imag, axis=0, keepdims=True)

    add_products(0, m_re, m_im, True)

    for copy in p_copies:
        copy.wait()
    for k in range(1, groups):
        mine += got[k - 1]
    a_re = take_lanes(mine[:, :width], own_index)
    a_im = take_lanes(mine[:, width:], own_index)
    h_re = jnp.where(present, kinetic * re + a_re, 0.0).astype(BF16)
    h_im = jnp.where(present, kinetic * im + a_im, 0.0).astype(BF16)
    out_ref[0, 0] = h_re
    out_ref[1, 0] = h_im
    add_products(2, h_re.astype(F32), h_im.astype(F32), False)

    ones = jnp.full((8, width), 1.0 / float(4 * radius * radius), F32)
    row = lax.dot_general(
        ones, sums[...], NT, preferred_element_type=F32, precision=lax.Precision.HIGHEST
    )
    message[...] = row[:1]
    inbox[pl.ds(me, 1), 0, :] = row[:1]

    @pl.loop(1, total)
    def _(k):
        pltpu.make_async_remote_copy(
            src_ref=message,
            dst_ref=inbox.at[me],
            send_sem=m_send,
            recv_sem=m_recv,
            device_id=where_is(lax.rem(me + k, total)),
            device_id_type=MESH,
        ).start()

    everyone = inbox.at[pl.ds(0, total - 1)]
    pltpu.make_async_copy(everyone, everyone, m_recv).wait()
    pltpu.make_async_copy(everyone, everyone, m_send).wait()

    rows = inbox[0:bands, 0, :]
    for g in range(1, groups):
        rows += inbox[g * bands : (g + 1) * bands, 0, :]
    unit = (
        lax.broadcasted_iota(jnp.int32, (msg_width, msg_width), 0)
        == lax.broadcasted_iota(jnp.int32, (msg_width, msg_width), 1)
    ).astype(F32)
    turned = lax.dot_general(
        unit, rows, NT, preferred_element_type=F32, precision=lax.Precision.HIGHEST
    )
    place_i = lax.broadcasted_iota(jnp.int32, (bands, bands), 0)
    place_j = lax.broadcasted_iota(jnp.int32, (bands, bands), 1)
    direct = lax.rem(place_j - place_i + bands, bands) <= half

    def assemble(c, sign):
        part_of = slice(c * bands, (c + 1) * bands)
        return jnp.where(direct, turned[part_of], sign * rows[:, part_of])

    corr_ref[0] = assemble(0, 1.0)
    corr_ref[1] = assemble(1, -1.0)
    red_ref[0] = assemble(2, 1.0)
    red_ref[1] = assemble(3, -1.0)


def body(bands, groups, orbitals, potential, slot_sticks, stick_entries):
    points = potential.shape[1]
    planes = potential.shape[0]
    width = stick_entries.shape[1]
    radius = width // 2
    slots = orbitals.shape[2]
    plane_pad = -(-planes // 128) * 128
    coarse = 2 * width
    sum_rows = -(-4 * bands // 128) * 128
    tz, tx, ty, tr = tables(points, width, radius, groups, planes, plane_pad, coarse)
    vmem = pl.BlockSpec(memory_space=pltpu.VMEM)
    hbm = pl.BlockSpec(memory_space=pltpu.HBM)
    total = bands * groups
    dma = pltpu.SemaphoreType.DMA
    return pl.pallas_call(
        functools.partial(kernel, bands, groups, points, radius),
        out_shape=(
            pltpu.VMEM(orbitals.shape, BF16),
            pltpu.VMEM((2, bands, bands), F32),
            pltpu.VMEM((2, bands, bands), F32),
        ),
        in_specs=[hbm] * 8,
        out_specs=(vmem, vmem, vmem),
        scratch_shapes=[
            pltpu.VMEM(orbitals.shape, BF16),
            pltpu.VMEM(slot_sticks.shape, jnp.int32),
            pltpu.VMEM((slots, width), jnp.int32),
            pltpu.VMEM(tz.shape[1:], BF16),
            pltpu.VMEM(tx.shape, BF16),
            pltpu.VMEM(ty.shape, BF16),
            pltpu.VMEM(tr.shape, BF16),
            pltpu.VMEM((plane_pad, points), F32),
            pltpu.VMEM((groups, slots, 2 * width), BF16),
            pltpu.VMEM((2, 2 * width, plane_pad), BF16),
            pltpu.VMEM((groups - 1, slots, 2 * width), F32),
            pltpu.VMEM((groups - 1, slots, 2 * width), F32),
            pltpu.VMEM((bands // 2 + 1, 2, slots, width), BF16),
            pltpu.VMEM((sum_rows, width), F32),
            pltpu.VMEM((1, sum_rows), F32),
            pltpu.VMEM((total, 1, sum_rows), F32),
            dma((8,)),
            dma((groups - 1,)),
            dma((groups - 1,)),
            dma((groups - 1,)),
            dma((groups - 1,)),
            dma((bands // 2 + 1,)),
            dma((bands // 2 + 1,)),
            dma,
            dma,
        ],
        compiler_params=pltpu.CompilerParams(
            collective_id=0, has_side_effects=True, vmem_limit_bytes=60000000
        ),
    )(orbitals, slot_sticks, stick_entries, potential, tz, tx, ty, tr)


def solution(mesh):
    bands = mesh.shape["band"]
    groups = mesh.shape["ga"]
    return jax.shard_map(
        functools.partial(body, bands, groups),
        mesh=mesh,
        in_specs=(P(None, "band", "ga", None), P("ga", None), P(), P()),
        out_specs=(P(None, "band", "ga", None), P(), P()),
        check_vma=False,
    )
```

profile of v0, /device:TPU:0, one launch (start us, length us, event | category | flops | bytes accessed | tf_op | source)
XLA Modules:
  0.0 26.5 jit_solution(16356459419194000375)
XLA Ops:
  0.6 24.0 %shard_map.103 = (bf16[2,1,80,128]{3,2,1,0:T(8,128)(2,1)S(1)}, f32[2,16,16]{2,1,0:T(8,128)S(1)}, f32[2,16,16]{2,1,0:T(8,128)S(1)}) custom-call(bf16[2,1,80,128]{3,2,1,0:T(8,128)(2,1)} %orb_hbm.1, s32[160]{0:T(256)} %slots_hbm.1, s32[160,128]{1,0:T(8,128)} %entries_hbm.1, f32[240,480]{1,0:T(8,128)} %pot_hbm.1, bf16[2,2,256,512]{3,2,1,0:T(8,128)(2,1)} %constant.8.clone.tz_hbm, ...), custom_call_target="tpu_custom_call" | custom-call | tf_op jit(solution)/shard_map/pallas_call | solution.py:372
  24.7 0.6 %copy.14 = bf16[2,1,80,128]{3,2,1,0:T(8,128)(2,1)} copy(bf16[2,1,80,128]{3,2,1,0:T(8,128)(2,1)S(1)} %get-tuple-element.3) | data formatting | bytes 81920
  25.3 0.6 %copy.15 = f32[2,16,16]{2,1,0:T(8,128)} copy(f32[2,16,16]{2,1,0:T(8,128)S(1)} %get-tuple-element.4) | data formatting | bytes 4096
  25.9 0.6 %copy.16 = f32[2,16,16]{2,1,0:T(8,128)} copy(f32[2,16,16]{2,1,0:T(8,128)S(1)} %get-tuple-element.5) | data formatting | bytes 4096
where the time goes:
time: 26.7 us; the launch traced here: 26.5 us
  Pallas kernels  24 us (90%)
  local copies, waits for them, and re-layouts  1.83 us (7%)
  between operations  0.64 us (2%)
    pallas_call x1, Pallas kernels, body(): pl.pallas_call(functools.partial(kernel, bands, groups, points, radius),...  24 us
    unnamed x3, local copies, waits for them, and re-layouts  1.83 us

commit v1 on v0

v1 whole, which is shorter than its diff:
```python
import functools
import math

import jax
import jax.numpy as jnp
import numpy as np
from jax import lax
from jax.experimental import pallas as pl
from jax.experimental.pallas import tpu as pltpu
from jax.sharding import PartitionSpec as P

MESH = pl.DeviceIdType.MESH
NT = (((1,), (1,)), ((), ()))
BF16 = jnp.bfloat16
F32 = jnp.float32
BLOCK = 4
UNROLL = 8


def split_np(table):
    high = table.astype(np.float32).astype(BF16)
    low = (table - high.astype(np.float64)).astype(np.float32).astype(BF16)
    return np.stack([high, low])


def tables(points, width, radius, groups, planes, plane_pad, coarse):
    freq = np.arange(width) - radius + 1
    used = (np.arange(width) < width - 1).astype(np.float64)
    z_tabs = []
    for group in range(groups):
        z = np.arange(planes) + group * planes
        angle = 2.0 * np.pi * ((freq[:, None] * z[None, :]) % points) / points
        cos = np.zeros((width, plane_pad))
        sin = np.zeros((width, plane_pad))
        cos[:, :planes] = np.cos(angle) * used[:, None]
        sin[:, :planes] = np.sin(angle) * used[:, None]
        z_tabs.append(split_np(np.block([[cos, sin], [-sin, cos]])))
    x = np.arange(coarse)
    angle = 2.0 * np.pi * ((freq[None, :] * x[:, None]) % coarse) / coarse
    cos = np.cos(angle) * used[None, :]
    sin = np.sin(angle) * used[None, :]
    forward = np.block([[cos, -sin], [sin, cos]])
    limit = 2 * (radius - 1)
    offset = (x[:, None] * points - np.arange(points)[None, :] * coarse) % (coarse * points)
    base = 2.0 * np.pi * offset / (coarse * points)
    resample = np.ones((coarse, points))
    for g in range(1, limit + 1):
        resample += 2.0 * np.cos(g * base)
    resample /= points
    return (
        np.stack(z_tabs),
        split_np(forward),
        split_np(forward.T.copy()),
        split_np(resample),
    )


def split(value):
    high = value.astype(BF16)
    low = (value - high.astype(F32)).astype(BF16)
    return high, low


def dot(a, b):
    return jnp.dot(a, b, preferred_element_type=F32)


def dot_nt(a, b):
    return lax.dot_general(a, b, NT, preferred_element_type=F32)


def take_lanes(value, index):
    return jnp.take_along_axis(value, index, axis=1, mode="promise_in_bounds")


def kernel(
    bands,
    groups,
    points,
    radius,
    orb_hbm,
    slots_hbm,
    entries_hbm,
    pot_hbm,
    tz_hbm,
    tx_hbm,
    ty_hbm,
    tr_hbm,
    out_ref,
    corr_ref,
    red_ref,
    orb_ref,
    slots_ref,
    entries_ref,
    tz,
    tx,
    ty,
    tr,
    pot,
    ent_t,
    inv_ref,
    raw,
    spread,
    colbuf,
    part,
    got,
    dense_ref,
    pdense,
    inbox_m,
    inbox_p,
    left_f,
    right_f,
    message,
    inbox_s,
    load_sem,
    near_sem,
    s_send,
    s_recv,
    x_send,
    x_recv,
    m_send,
    m_recv,
    p_send,
    p_recv,
    b_send,
    b_recv,
):
    band = lax.axis_index("band")
    ga = lax.axis_index("ga")
    total = bands * groups
    me = ga * bands + band
    slots = orb_hbm.shape[2]
    width = orb_hbm.shape[3]
    planes = pot_hbm.shape[0]
    plane_pad = pot.shape[0]
    coarse = ty.shape[2] // 2
    reducers = inbox_s.shape[0]
    rows = width // reducers
    per_group = reducers // groups
    block = math.gcd(bands, BLOCK)
    blocks = bands // block
    place = lax.rem(band, block)
    base = band - place
    first_band = bands // 2 - per_group + 1

    loads = [
        pltpu.make_async_copy(entries_hbm, entries_ref, load_sem.at[5]),
        pltpu.make_async_copy(orb_hbm, orb_ref, load_sem.at[6]),
        pltpu.make_async_copy(slots_hbm, slots_ref, load_sem.at[7]),
        pltpu.make_async_copy(pot_hbm, pot.at[pl.ds(0, planes)], load_sem.at[0]),
        pltpu.make_async_copy(tr_hbm, tr, load_sem.at[1]),
        pltpu.make_async_copy(tz_hbm.at[ga], tz, load_sem.at[2]),
        pltpu.make_async_copy(tx_hbm, tx, load_sem.at[3]),
        pltpu.make_async_copy(ty_hbm, ty, load_sem.at[4]),
    ]
    load_entries, load_orb, load_slots, load_pot, load_tr, load_tz, load_tx, load_ty = loads
    load_orb.start()

    has_low = band >= block
    has_high = band < bands - block
    barrier = pltpu.get_barrier_semaphore()
    for g in range(groups):
        for c in range(block):
            if g or c:
                pl.semaphore_signal(
                    barrier,
                    inc=1,
                    device_id=(base + lax.rem(place + c, block), lax.rem(ga + g, groups)),
                    device_id_type=MESH,
                )

    def near(semaphore_low, semaphore_high):
        @pl.when(has_low)
        def _():
            pl.semaphore_signal(
                semaphore_high, inc=1, device_id=(band - block, ga), device_id_type=MESH
            )

        @pl.when(has_high)
        def _():
            pl.semaphore_signal(
                semaphore_low, inc=1, device_id=(band + block, ga), device_id_type=MESH
            )

    def near_wait():
        @pl.when(has_low)
        def _():
            pl.semaphore_wait(near_sem.at[0], 1)

        @pl.when(has_high)
        def _():
            pl.semaphore_wait(near_sem.at[1], 1)

    near(barrier, barrier)
    for load in loads:
        if load is not load_orb:
            load.start()
    if plane_pad > planes:
        pot[pl.ds(planes, plane_pad - planes), :] = jnp.zeros(
            (plane_pad - planes, pot.shape[1]), F32
        )

    load_orb.wait()
    pl.semaphore_wait(
        barrier, block * groups - 1 + has_low.astype(jnp.int32) + has_high.astype(jnp.int32)
    )
    s_copies = []
    for k in range(1, groups):
        copy = pltpu.make_async_remote_copy(
            src_ref=orb_ref.at[:, 0],
            dst_ref=raw.at[k - 1],
            send_sem=s_send.at[k - 1],
            recv_sem=s_recv.at[k - 1],
            device_id=(band, lax.rem(ga + k, groups)),
            device_id_type=MESH,
        )
        copy.start()
        s_copies.append(copy)
    near(near_sem.at[0], near_sem.at[1])

    load_entries.wait()
    load_slots.wait()
    all_slots = groups * slots
    listed = entries_ref[...].astype(F32)
    slot_pad = ent_t.shape[1] - all_slots
    if slot_pad:
        listed = jnp.concatenate([listed, jnp.full((slot_pad, width), -1.0, F32)], axis=0)
    ent_t[...] = listed.T
    lanes = ent_t.shape[1]
    which = lax.broadcasted_iota(jnp.int32, (width, lanes), 0).astype(F32).astype(BF16)

    def invert(step, found):
        for u in range(UNROLL):
            k = step * UNROLL + u
            row = jnp.broadcast_to(ent_t[pl.ds(k, 1), :], (16, lanes)).astype(BF16)
            row = jnp.concatenate([row] * (width // 16), axis=0)
            found = jnp.where(row == which, k.astype(F32).astype(BF16), found)
        return found

    found = lax.fori_loop(
        0, width // UNROLL, invert, jnp.full((width, lanes), -1.0, BF16)
    )
    found = found.astype(F32).T.astype(jnp.int32)
    for g in range(groups):
        inv_ref[g] = found[g * slots : (g + 1) * slots]

    def spread_of(g, re, im):
        inverse = inv_ref[g]
        filled = inverse >= 0
        index = jnp.maximum(inverse, 0)
        spread[g, :, :width] = jnp.where(filled, take_lanes(re, index), 0.0).astype(BF16)
        spread[g, :, width:] = jnp.where(filled, take_lanes(im, index), 0.0).astype(BF16)

    re = orb_ref[0, 0].astype(F32)
    im = orb_ref[1, 0].astype(F32)
    spread_of(ga, re, im)

    near_wait()
    rounds = max(blocks // 2, 1)
    if rounds > 1:
        near(near_sem.at[0], near_sem.at[1])

    load_pot.wait()
    load_tr.wait()
    pot_hi, pot_lo = split(pot[...])
    weight = dot_nt(tr[0], pot_hi) + dot_nt(tr[0], pot_lo) + dot_nt(tr[1], pot_hi)

    for k, copy in enumerate(s_copies, 1):
        copy.wait()
        spread_of(
            lax.rem(ga - k + groups, groups), raw[k - 1, 0].astype(F32), raw[k - 1, 1].astype(F32)
        )
    all_sticks = slots_ref[...].reshape(1, all_slots)
    sticks = [all_sticks[:, g * slots : (g + 1) * slots] for g in range(groups)]
    dense = jnp.zeros((width, 2 * width), F32)
    sub = lax.broadcasted_iota(jnp.int32, (width, slots), 0)
    for g in range(groups):
        choose = jnp.where(sub == sticks[g], 1.0, 0.0).astype(BF16)
        dense += dot(choose, spread[g])
    dense = dense.astype(BF16)
    dense_ref[...] = dense

    for r in range(1, rounds):
        near_wait()
        if r < rounds - 1:
            near(near_sem.at[0], near_sem.at[1])

    def place_of(r):
        return first_band + 2 * (r % per_group), r // per_group

    def m_copy(q):
        start = pl.multiple_of((ga * per_group + q) * rows, rows)
        return pltpu.make_async_remote_copy(
            src_ref=dense_ref.at[pl.ds(start, rows)],
            dst_ref=inbox_m.at[band],
            send_sem=m_send.at[q],
            recv_sem=m_recv,
            device_id=(first_band + 2 * q, ga),
            device_id_type=MESH,
        )

    def m_each(act, own):
        for q in range(per_group):
            mine = band == first_band + 2 * q

            @pl.when(jnp.logical_not(mine))
            def _(q=q):
                act(m_copy(q))

            if own:

                @pl.when(mine)
                def _(q=q):
                    start = pl.multiple_of((ga * per_group + q) * rows, rows)
                    inbox_m[band] = dense_ref[pl.ds(start, rows), :]

    m_each(lambda copy: copy.start(), True)

    load_tz.wait()
    columns = dot(dense, tz[0]) + dot(dense, tz[1])
    col_hi, col_lo = split(columns)
    colbuf[0, :width] = col_hi[:, :plane_pad]
    colbuf[0, width:] = col_hi[:, plane_pad:]
    colbuf[1, :width] = col_lo[:, :plane_pad]
    colbuf[1, width:] = col_lo[:, plane_pad:]
    load_tx.wait()
    field = dot(tx[0], colbuf[0]) + dot(tx[0], colbuf[1]) + dot(tx[1], colbuf[0])
    product = jnp.concatenate([field[:coarse] * weight, field[coarse:] * weight], axis=0)
    pro_hi, pro_lo = split(product)
    load_ty.wait()
    back = dot(ty[0], pro_hi) + dot(ty[0], pro_lo) + dot(ty[1], pro_hi)
    back = jnp.concatenate([back[:width], back[width:]], axis=1)
    back_hi, back_lo = split(back)
    spectra = dot_nt(back_hi, tz[0]) + dot_nt(back_hi, tz[1]) + dot_nt(back_lo, tz[0])
    spectra = spectra * (1.0 / float(points * coarse))
    spec_hi, spec_lo = split(spectra)
    pdense[...] = spec_hi

    def p_copy(r):
        return pltpu.make_async_remote_copy(
            src_ref=pdense.at[pl.ds(r * rows, rows)],
            dst_ref=inbox_p.at[me],
            send_sem=p_send.at[r],
            recv_sem=p_recv,
            device_id=place_of(r),
            device_id_type=MESH,
        )

    def p_each(act, own):
        for r in range(reducers):
            to_band, to_ga = place_of(r)
            mine = me == to_ga * bands + to_band

            @pl.when(jnp.logical_not(mine))
            def _(r=r):
                act(p_copy(r))

            if own:

                @pl.when(mine)
                def _(r=r):
                    inbox_p[me] = pdense[pl.ds(r * rows, rows), :]

    p_each(lambda copy: copy.start(), True)

    eye = lax.broadcasted_iota(jnp.int32, (slots, slots), 0) == lax.broadcasted_iota(
        jnp.int32, (slots, slots), 1
    )

    def stick_column(g):
        row = sticks[0]
        for other in range(1, groups):
            row = jnp.where(g == other, sticks[other], row)
        row = row.astype(F32)
        return jnp.sum(jnp.where(eye, row, 0.0), axis=1, keepdims=True)

    lane = lax.broadcasted_iota(jnp.int32, (slots, width), 1)
    lane_f = lane.astype(F32)
    x_copies = []
    for k in range(1, groups + 1):
        target = lax.rem(ga + k, groups)
        stick = stick_column(target)
        choose = jnp.where(stick == lane_f, 1.0, 0.0).astype(BF16)
        mine = dot(choose, spec_hi) + dot(choose, spec_lo)
        if k < groups:
            part[k - 1] = mine
            copy = pltpu.make_async_remote_copy(
                src_ref=part.at[k - 1],
                dst_ref=got.at[k - 1],
                send_sem=x_send.at[k - 1],
                recv_sem=x_recv.at[k - 1],
                device_id=(band, target),
                device_id_type=MESH,
            )
            copy.start()
            x_copies.append(copy)

    own = entries_ref[pl.ds(pl.multiple_of(ga * slots, 8), slots)]
    present = own >= 0
    gx = stick - float(radius - 1)
    gz = (own - (radius - 1)).astype(F32)
    kinetic = (gx * gx + gz * gz) * (1.0 / float(radius * radius))
    own_index = jnp.maximum(own, 0)

    for copy in x_copies:
        copy.wait()
    for k in range(1, groups):
        mine += got[k - 1]
    a_re = take_lanes(mine[:, :width], own_index)
    a_im = take_lanes(mine[:, width:], own_index)
    out_ref[0, 0] = jnp.where(present, kinetic * re + a_re, 0.0).astype(BF16)
    out_ref[1, 0] = jnp.where(present, kinetic * im + a_im, 0.0).astype(BF16)

    offset = band - first_band
    is_reducer = (offset >= 0) & (offset < 2 * per_group) & (lax.rem(offset + 2 * bands, 2) == 0)
    number = ga * per_group + lax.div(jnp.clip(offset, 0, 2 * per_group - 1), 2)

    def b_copy(t):
        return pltpu.make_async_remote_copy(
            src_ref=message,
            dst_ref=inbox_s.at[number],
            send_sem=b_send.at[t],
            recv_sem=b_recv,
            device_id=(t // groups, t % groups) if isinstance(t, int) else (lax.div(t, groups), lax.rem(t, groups)),
            device_id_type=MESH,
        )

    def b_each(act):
        order = band * groups + ga
        if total <= 64:
            for t in range(total):

                @pl.when(order != t)
                def _(t=t):
                    act(b_copy(t))
        else:

            @pl.loop(0, total)
            def _(t):
                @pl.when(order != t)
                def _():
                    act(b_copy(t))

    @pl.when(is_reducer)
    def _():
        m_all = inbox_m.at[pl.ds(0, bands - 1)]
        pltpu.make_async_copy(m_all, m_all, m_recv).wait()
        left = inbox_m[...].astype(F32)
        for c in range(2):
            left_f[c] = left[:, :, c * width : (c + 1) * width].reshape(bands * rows, width)
        row_id = lax.broadcasted_iota(jnp.int32, (rows, 2 * width), 0) + number * rows
        lane_id = lax.broadcasted_iota(jnp.int32, (rows, 2 * width), 1)
        row_f = (row_id - (radius - 1)).astype(F32)
        lane_g = (jnp.where(lane_id >= width, lane_id - width, lane_id) - (radius - 1)).astype(F32)
        kin = (row_f * row_f + lane_g * lane_g) * (1.0 / float(radius * radius))
        right = left * kin[None]
        p_all = inbox_p.at[pl.ds(0, total - 1)]
        pltpu.make_async_copy(p_all, p_all, p_recv).wait()
        for g in range(groups):
            right += inbox_p[g * bands : (g + 1) * bands].astype(F32)
        for c in range(2):
            right_f[c] = right[:, :, c * width : (c + 1) * width].reshape(bands * rows, width)
        result = jnp.zeros((bands, 4 * bands), F32)
        for r in range(rows):
            every = pl.ds(r, bands, stride=rows)
            low_re, low_im = left_f[0, every, :], left_f[1, every, :]
            high_re, high_im = right_f[0, every, :], right_f[1, every, :]
            low = jnp.concatenate([low_re, low_im], axis=1)
            stack = jnp.concatenate(
                [
                    jnp.concatenate([high_re, high_im], axis=1),
                    jnp.concatenate([high_im, -high_re], axis=1),
                    low,
                    jnp.concatenate([low_im, -low_re], axis=1),
                ],
                axis=0,
            )
            result += dot_nt(low.astype(BF16), stack.astype(BF16))
        result = result * (1.0 / float(4 * radius * radius))
        fold = message.shape[1] // (4 * bands)
        depth = message.shape[0]
        message[...] = jnp.concatenate(
            [result[f * depth : (f + 1) * depth] for f in range(fold)], axis=1
        )
        inbox_s[number] = message[...]
        b_each(lambda copy: copy.start())
        most = inbox_s.at[pl.ds(0, reducers - 1)]
        pltpu.make_async_copy(most, most, b_recv).wait()

    @pl.when(jnp.logical_not(is_reducer))
    def _():
        pltpu.make_async_copy(inbox_s, inbox_s, b_recv).wait()

    final = inbox_s[0]
    for r in range(1, reducers):
        final += inbox_s[r]
    span = 4 * bands
    fold = message.shape[1] // span
    final = jnp.concatenate([final[:, f * span : (f + 1) * span] for f in range(fold)], axis=0)
    red_ref[0] = final[:, :bands]
    red_ref[1] = final[:, bands : 2 * bands]
    corr_ref[0] = final[:, 2 * bands : 3 * bands]
    corr_ref[1] = final[:, 3 * bands :]

    m_each(lambda copy: copy.wait_send(), False)
    p_each(lambda copy: copy.wait_send(), False)

    @pl.when(is_reducer)
    def _():
        b_each(lambda copy: copy.wait_send())


def write_out(out_ref, corr_ref, red_ref, out_hbm, corr_hbm, red_hbm, sem):
    copies = [
        pltpu.make_async_copy(out_ref, out_hbm, sem.at[0]),
        pltpu.make_async_copy(corr_ref, corr_hbm, sem.at[1]),
        pltpu.make_async_copy(red_ref, red_hbm, sem.at[2]),
    ]
    for copy in copies:
        copy.start()
    for copy in copies:
        copy.wait()


def body(bands, groups, orbitals, potential, slot_sticks, stick_entries):
    points = potential.shape[1]
    planes = potential.shape[0]
    width = stick_entries.shape[1]
    radius = width // 2
    slots = orbitals.shape[2]
    plane_pad = -(-planes // 128) * 128
    coarse = 2 * width
    reducers = width // 16
    per_group = reducers // groups
    rows = width // reducers
    fold = max(1, 128 // (4 * bands))
    slot_lanes = -(-groups * slots // 128) * 128
    tz, tx, ty, tr = tables(points, width, radius, groups, planes, plane_pad, coarse)
    vmem = pl.BlockSpec(memory_space=pltpu.VMEM)
    hbm = pl.BlockSpec(memory_space=pltpu.HBM)
    total = bands * groups
    dma = pltpu.SemaphoreType.DMA
    results = pl.pallas_call(
        functools.partial(kernel, bands, groups, points, radius),
        out_shape=(
            pltpu.VMEM(orbitals.shape, BF16),
            pltpu.VMEM((2, bands, bands), F32),
            pltpu.VMEM((2, bands, bands), F32),
        ),
        in_specs=[hbm] * 8,
        out_specs=(vmem, vmem, vmem),
        scratch_shapes=[
            pltpu.VMEM(orbitals.shape, BF16),
            pltpu.VMEM(slot_sticks.shape, jnp.int32),
            pltpu.VMEM(stick_entries.shape, jnp.int32),
            pltpu.VMEM(tz.shape[1:], BF16),
            pltpu.VMEM(tx.shape, BF16),
            pltpu.VMEM(ty.shape, BF16),
            pltpu.VMEM(tr.shape, BF16),
            pltpu.VMEM((plane_pad, points), F32),
            pltpu.VMEM((width, slot_lanes), F32),
            pltpu.VMEM((groups, slots, width), jnp.int32),
            pltpu.VMEM((groups - 1, 2, slots, width), BF16),
            pltpu.VMEM((groups, slots, 2 * width), BF16),
            pltpu.VMEM((2, 2 * width, plane_pad), BF16),
            pltpu.VMEM((groups - 1, slots, 2 * width), F32),
            pltpu.VMEM((groups - 1, slots, 2 * width), F32),
            pltpu.VMEM((width, 2 * width), BF16),
            pltpu.VMEM((width, 2 * width), BF16),
            pltpu.VMEM((bands, rows, 2 * width), BF16),
            pltpu.VMEM((total, rows, 2 * width), BF16),
            pltpu.VMEM((2, bands * rows, width), F32),
            pltpu.VMEM((2, bands * rows, width), F32),
            pltpu.VMEM((bands // fold, 4 * bands * fold), F32),
            pltpu.VMEM((reducers, bands // fold, 4 * bands * fold), F32),
            dma((8,)),
            pltpu.SemaphoreType.REGULAR((2,)),
            dma((groups - 1,)),
            dma((groups - 1,)),
            dma((groups - 1,)),
            dma((groups - 1,)),
            dma((per_group,)),
            dma,
            dma((reducers,)),
            dma,
            dma((total,)),
            dma,
        ],
        compiler_params=pltpu.CompilerParams(
            collective_id=0, has_side_effects=True, vmem_limit_bytes=60000000
        ),
    )(orbitals, slot_sticks, stick_entries, potential, tz, tx, ty, tr)
    return pl.pallas_call(
        write_out,
        out_shape=[jax.ShapeDtypeStruct(r.shape, r.dtype) for r in results],
        in_specs=[vmem] * 3,
        out_specs=[hbm] * 3,
        scratch_shapes=[dma((3,))],
    )(*results)


def solution(mesh):
    bands = mesh.shape["band"]
    groups = mesh.shape["ga"]
    return jax.shard_map(
        functools.partial(body, bands, groups),
        mesh=mesh,
        in_specs=(P(None, "band", "ga", None), P("ga", None), P(), P()),
        out_specs=(P(None, "band", "ga", None), P(), P()),
        check_vma=False,
    )
```

time: 26.7 us -> 23.1 us (0.87)
  Pallas kernels: 24 us -> 20.4 us
    pallas_call x1, Pallas kernels: 24 us -> 19 us  [body(): pl.pallas_call(functools.partial(kernel, bands, groups, points, radius),...]
    pallas_call x0 -> x1, Pallas kernels: none -> 1.45 us  [body(): pl.pallas_call(write_out, out_shape=[jax.ShapeDtypeStruct(r.shape, r.dtyp...]
    unnamed x3 -> x6, local copies, waits for them, and re-layouts: 1.83 us -> 1.8 us
where the time goes in v1:
time: 23.1 us; the launch traced here: 22.9 us
  Pallas kernels  20.4 us (88%)
  local copies, waits for them, and re-layouts  1.8 us (8%)
  between operations  0.65 us (3%)
    pallas_call x1, Pallas kernels, body(): pl.pallas_call(functools.partial(kernel, bands, groups, points, radius),...  19 us
    unnamed x6, local copies, waits for them, and re-layouts  1.8 us
    pallas_call x1, Pallas kernels, body(): pl.pallas_call(write_out, out_shape=[jax.ShapeDtypeStruct(r.shape, r.dtyp...  1.45 us

profile of v1, /device:TPU:0, one launch (start us, length us, event | category | flops | bytes accessed | tf_op | source)
XLA Modules:
  0.0 22.9 jit_solution(8045248497843841004)
XLA Ops:
  0.6 19.0 %shard_map.103 = (bf16[2,1,80,128]{3,2,1,0:T(8,128)(2,1)S(1)}, f32[2,16,16]{2,1,0:T(8,128)S(1)}, f32[2,16,16]{2,1,0:T(8,128)S(1)}) custom-call(bf16[2,1,80,128]{3,2,1,0:T(8,128)(2,1)} %orb_hbm.1, s32[160]{0:T(256)} %slots_hbm.1, s32[160,128]{1,0:T(8,128)} %entries_hbm.1, f32[240,480]{1,0:T(8,128)} %pot_hbm.1, bf16[2,2,256,512]{3,2,1,0:T(8,128)(2,1)} %constant.8.clone.tz_hbm, ...), custom_call_target="tpu_custom_call" | custom-call | tf_op jit(solution)/shard_map/pallas_call | solution.py:543
  19.6 0.0 copy-start
  19.6 0.6 %copy-done = bf16[2,1,80,128]{3,2,1,0:T(8,128)(2,1)} copy-done((bf16[2,1,80,128]{3,2,1,0:T(8,128)(2,1)}, bf16[2,1,80,128]{3,2,1,0:T(8,128)(2,1)S(1)}, u32[]{:S(2)}) %copy-start) | copy-done | bytes 40984
  20.2 0.0 copy-start.1
  20.2 0.6 %copy-done.1 = f32[2,16,16]{2,1,0:T(8,128)} copy-done((f32[2,16,16]{2,1,0:T(8,128)}, f32[2,16,16]{2,1,0:T(8,128)S(1)}, u32[]{:S(2)}) %copy-start.1) | copy-done | bytes 2072
  20.8 0.0 copy-start.2
  20.8 0.6 %copy-done.2 = f32[2,16,16]{2,1,0:T(8,128)} copy-done((f32[2,16,16]{2,1,0:T(8,128)}, f32[2,16,16]{2,1,0:T(8,128)S(1)}, u32[]{:S(2)}) %copy-start.2) | copy-done | bytes 2072
  21.4 1.4 %shard_map.104 = (bf16[2,1,80,128]{3,2,1,0:T(8,128)(2,1)}, f32[2,16,16]{2,1,0:T(8,128)}, f32[2,16,16]{2,1,0:T(8,128)}) custom-call(bf16[2,1,80,128]{3,2,1,0:T(8,128)(2,1)} %copy-done, f32[2,16,16]{2,1,0:T(8,128)} %copy-done.1, f32[2,16,16]{2,1,0:T(8,128)} %copy-done.2), custom_call_target="tpu_custom_call" | custom-call | tf_op jit(solution)/shard_map/pallas_call | solution.py:593
Async XLA Ops:
  19.6 0.6 %copy-start = (bf16[2,1,80,128]{3,2,1,0:T(8,128)(2,1)}, bf16[2,1,80,128]{3,2,1,0:T(8,128)(2,1)S(1)}, u32[]{:S(2)}) copy-start(bf16[2,1,80,128]{3,2,1,0:T(8,128)(2,1)S(1)} %get-tuple-element.6.out_ref) | copy-start | bytes 122884
  20.2 0.6 %copy-start.1 = (f32[2,16,16]{2,1,0:T(8,128)}, f32[2,16,16]{2,1,0:T(8,128)S(1)}, u32[]{:S(2)}) copy-start(f32[2,16,16]{2,1,0:T(8,128)S(1)} %get-tuple-element.7.corr_ref) | copy-start | bytes 6148
  20.8 0.6 %copy-start.2 = (f32[2,16,16]{2,1,0:T(8,128)}, f32[2,16,16]{2,1,0:T(8,128)S(1)}, u32[]{:S(2)}) copy-start(f32[2,16,16]{2,1,0:T(8,128)S(1)} %get-tuple-element.8.red_ref) | copy-start | bytes 6148

commit v2 on v1

--- a/solution.py
+++ b/solution.py
@@ -596,7 +596,7 @@
         in_specs=[vmem] * 3,
         out_specs=[hbm] * 3,
         scratch_shapes=[dma((3,))],
-    )(*results)
+    )(*[pltpu.with_memory_space_constraint(r, pltpu.VMEM) for r in results])
 
 
 def solution(mesh):

time: 23.1 us -> 20.4 us (0.88)
  local copies, waits for them, and re-layouts: 1.8 us -> 0 us
  Pallas kernels: 20.4 us -> 19.6 us
    unnamed x6 -> x0, local copies, waits for them, and re-layouts: 1.8 us -> none
    pallas_call x1, Pallas kernels: 1.45 us -> 0.65 us  [body(): pl.pallas_call(write_out, out_shape=[jax.ShapeDtypeStruct(r.shape, r.dtyp...]
where the time goes in v2:
time: 20.4 us; the launch traced here: 20.3 us
  Pallas kernels  19.6 us (96%)
  between operations  0.64 us (3%)
    pallas_call x1, Pallas kernels, body(): pl.pallas_call(functools.partial(kernel, bands, groups, points, radius),...  19 us
    pallas_call x1, Pallas kernels, body(): pl.pallas_call(write_out, out_shape=[jax.ShapeDtypeStruct(r.shape, r.dtyp...  0.65 us

profile of v2, /device:TPU:0, one launch (start us, length us, event | category | flops | bytes accessed | tf_op | source)
XLA Modules:
  0.0 20.3 jit_solution(3541948144393167561)
XLA Ops:
  0.6 19.0 %shard_map.103 = (bf16[2,1,80,128]{3,2,1,0:T(8,128)(2,1)S(1)}, f32[2,16,16]{2,1,0:T(8,128)S(1)}, f32[2,16,16]{2,1,0:T(8,128)S(1)}) custom-call(bf16[2,1,80,128]{3,2,1,0:T(8,128)(2,1)} %orb_hbm.1, s32[160]{0:T(256)} %slots_hbm.1, s32[160,128]{1,0:T(8,128)} %entries_hbm.1, f32[240,480]{1,0:T(8,128)} %pot_hbm.1, bf16[2,2,256,512]{3,2,1,0:T(8,128)(2,1)} %constant.8.clone.tz_hbm, ...), custom_call_target="tpu_custom_call" | custom-call | tf_op jit(solution)/shard_map/pallas_call | solution.py:543
  19.6 0.7 %shard_map.104 = (bf16[2,1,80,128]{3,2,1,0:T(8,128)(2,1)}, f32[2,16,16]{2,1,0:T(8,128)}, f32[2,16,16]{2,1,0:T(8,128)}) custom-call(bf16[2,1,80,128]{3,2,1,0:T(8,128)(2,1)S(1)} %get-tuple-element.6.out_ref, f32[2,16,16]{2,1,0:T(8,128)S(1)} %get-tuple-element.7.corr_ref, f32[2,16,16]{2,1,0:T(8,128)S(1)} %get-tuple-element.8.red_ref), custom_call_target="tpu_custom_call" | custom-call | tf_op jit(solution)/shard_map/pallas_call | solution.py:593

commit v3 on v2

--- a/solution.py
+++ b/solution.py
@@ -21,6 +21,11 @@
     high = table.astype(np.float32).astype(BF16)
     low = (table - high.astype(np.float64)).astype(np.float32).astype(BF16)
     return np.stack([high, low])
+
+
+def triple(pair, axis):
+    high, low = (np.take(pair, i, axis=pair.ndim - 3) for i in range(2))
+    return np.concatenate([high, high, low], axis=axis)
 
 
 def tables(points, width, radius, groups, planes, plane_pad, coarse):
@@ -47,10 +52,12 @@
     for g in range(1, limit + 1):
         resample += 2.0 * np.cos(g * base)
     resample /= points
+    z_tabs = np.stack(z_tabs)
     return (
-        np.stack(z_tabs),
-        split_np(forward),
-        split_np(forward.T.copy()),
+        z_tabs.reshape(groups, 2 * z_tabs.shape[2], z_tabs.shape[3]),
+        triple(np.swapaxes(z_tabs, 2, 3), 1),
+        triple(split_np(forward), 1),
+        triple(split_np(forward.T.copy()), 1),
         split_np(resample),
     )
 
@@ -59,6 +66,11 @@
     high = value.astype(BF16)
     low = (value - high.astype(F32)).astype(BF16)
     return high, low
+
+
+def thirds(value, axis):
+    high, low = split(value)
+    return jnp.concatenate([high, low, high], axis=axis)
 
 
 def dot(a, b):
@@ -83,6 +95,7 @@
     entries_hbm,
     pot_hbm,
     tz_hbm,
+    tb_hbm,
     tx_hbm,
     ty_hbm,
     tr_hbm,
@@ -93,6 +106,7 @@
     slots_ref,
     entries_ref,
     tz,
+    tb,
     tx,
     ty,
     tr,
@@ -101,7 +115,6 @@
     inv_ref,
     raw,
     spread,
-    colbuf,
     part,
     got,
     dense_ref,
@@ -114,6 +127,7 @@
     inbox_s,
     load_sem,
     near_sem,
+    pair_sem,
     s_send,
     s_recv,
     x_send,
@@ -133,7 +147,7 @@
     width = orb_hbm.shape[3]
     planes = pot_hbm.shape[0]
     plane_pad = pot.shape[0]
-    coarse = ty.shape[2] // 2
+    coarse = tx.shape[0] // 2
     reducers = inbox_s.shape[0]
     rows = width // reducers
     per_group = reducers // groups
@@ -152,15 +166,16 @@
         pltpu.make_async_copy(tz_hbm.at[ga], tz, load_sem.at[2]),
         pltpu.make_async_copy(tx_hbm, tx, load_sem.at[3]),
         pltpu.make_async_copy(ty_hbm, ty, load_sem.at[4]),
+        pltpu.make_async_copy(tb_hbm.at[ga], tb, load_sem.at[8]),
     ]
-    load_entries, load_orb, load_slots, load_pot, load_tr, load_tz, load_tx, load_ty = loads
+    load_entries, load_orb, load_slots, load_pot, load_tr, load_tz, load_tx, load_ty, load_tb = loads
     load_orb.start()
 
     has_low = band >= block
     has_high = band < bands - block
     barrier = pltpu.get_barrier_semaphore()
-    for g in range(groups):
-        for c in range(block):
+    for c in range(block):
+        for g in range(groups):
             if g or c:
                 pl.semaphore_signal(
                     barrier,
@@ -286,7 +301,7 @@
             near(near_sem.at[0], near_sem.at[1])
 
     def place_of(r):
-        return first_band + 2 * (r % per_group), r // per_group
+        return first_band + 2 * lax.rem(r, per_group), lax.div(r, per_group)
 
     def m_copy(q):
         start = pl.multiple_of((ga * per_group + q) * rows, rows)
@@ -317,28 +332,43 @@
     m_each(lambda copy: copy.start(), True)
 
     load_tz.wait()
-    columns = dot(dense, tz[0]) + dot(dense, tz[1])
-    col_hi, col_lo = split(columns)
-    colbuf[0, :width] = col_hi[:, :plane_pad]
-    colbuf[0, width:] = col_hi[:, plane_pad:]
-    colbuf[1, :width] = col_lo[:, :plane_pad]
-    colbuf[1, width:] = col_lo[:, plane_pad:]
+    pair = jnp.concatenate([dense, dense], axis=1)
+    columns = [dot(pair, tz[:, :plane_pad]), dot(pair, tz[:, plane_pad:])]
+    columns = jnp.concatenate(columns, axis=0)
     load_tx.wait()
-    field = dot(tx[0], colbuf[0]) + dot(tx[0], colbuf[1]) + dot(tx[1], colbuf[0])
+    columns = thirds(columns, 0)
+    quarter = coarse // 2
+    field = jnp.concatenate(
+        [dot(tx[i * quarter : (i + 1) * quarter], columns) for i in range(4)], axis=0
+    )
     product = jnp.concatenate([field[:coarse] * weight, field[coarse:] * weight], axis=0)
-    pro_hi, pro_lo = split(product)
+    product = thirds(product, 0)
     load_ty.wait()
-    back = dot(ty[0], pro_hi) + dot(ty[0], pro_lo) + dot(ty[1], pro_hi)
-    back = jnp.concatenate([back[:width], back[width:]], axis=1)
-    back_hi, back_lo = split(back)
-    spectra = dot_nt(back_hi, tz[0]) + dot_nt(back_hi, tz[1]) + dot_nt(back_lo, tz[0])
+    back = jnp.concatenate([dot(ty[:width], product), dot(ty[width:], product)], axis=0)
+    back = thirds(jnp.concatenate([back[:width], back[width:]], axis=1), 1)
+    load_tb.wait()
+    spectra = dot(back, tb[...])
     spectra = spectra * (1.0 / float(points * coarse))
     spec_hi, spec_lo = split(spectra)
     pdense[...] = spec_hi
 
+    nearest = jnp.where(
+        band >= bands // 2, per_group // 2 + lax.div(lax.rem(band, block), 2), lax.div(lax.rem(band, block), 2)
+    )
+    nearest = lax.rem(nearest, per_group)
+
+    def far_reducer(far):
+        g = lax.rem(ga + far // per_group, groups)
+        q, bit = 0, 1
+        while bit < per_group:
+            own_bit = lax.rem(lax.div(nearest, bit), 2)
+            q = q + bit * (1 - own_bit if far % per_group & bit else own_bit)
+            bit *= 2
+        return g * per_group + q
+
     def p_copy(r):
         return pltpu.make_async_remote_copy(
-            src_ref=pdense.at[pl.ds(r * rows, rows)],
+            src_ref=pdense.at[pl.ds(pl.multiple_of(r * rows, rows), rows)],
             dst_ref=inbox_p.at[me],
             send_sem=p_send.at[r],
             recv_sem=p_recv,
@@ -347,7 +377,8 @@
         )
 
     def p_each(act, own):
-        for r in range(reducers):
+        for far in reversed(range(reducers)):
+            r = far_reducer(far)
             to_band, to_ga = place_of(r)
             mine = me == to_ga * bands + to_band
 
@@ -359,9 +390,13 @@
 
                 @pl.when(mine)
                 def _(r=r):
-                    inbox_p[me] = pdense[pl.ds(r * rows, rows), :]
+                    inbox_p[me] = pdense[pl.ds(pl.multiple_of(r * rows, rows), rows), :]
 
     p_each(lambda copy: copy.start(), True)
+
+    @pl.when(lax.rem(band, 2) == 0)
+    def _():
+        pl.semaphore_signal(pair_sem, inc=1, device_id=(band + 1, ga), device_id_type=MESH)
 
     eye = lax.broadcasted_iota(jnp.int32, (slots, slots), 0) == lax.broadcasted_iota(
         jnp.int32, (slots, slots), 1
@@ -392,7 +427,6 @@
                 device_id=(band, target),
                 device_id_type=MESH,
             )
-            copy.start()
             x_copies.append(copy)
 
     own = entries_ref[pl.ds(pl.multiple_of(ga * slots, 8), slots)]
@@ -402,17 +436,15 @@
     kinetic = (gx * gx + gz * gz) * (1.0 / float(radius * radius))
     own_index = jnp.maximum(own, 0)
 
+    @pl.when(lax.rem(band, 2) == 1)
+    def _():
+        pl.semaphore_wait(pair_sem, 1)
+
     for copy in x_copies:
-        copy.wait()
-    for k in range(1, groups):
-        mine += got[k - 1]
-    a_re = take_lanes(mine[:, :width], own_index)
-    a_im = take_lanes(mine[:, width:], own_index)
-    out_ref[0, 0] = jnp.where(present, kinetic * re + a_re, 0.0).astype(BF16)
-    out_ref[1, 0] = jnp.where(present, kinetic * im + a_im, 0.0).astype(BF16)
+        copy.start()
 
     offset = band - first_band
-    is_reducer = (offset >= 0) & (offset < 2 * per_group) & (lax.rem(offset + 2 * bands, 2) == 0)
+    is_reducer = (offset >= 0) & (offset < 2 * per_group) & (lax.rem(band + 1, 2) == 0)
     number = ga * per_group + lax.div(jnp.clip(offset, 0, 2 * per_group - 1), 2)
 
     def b_copy(t):
@@ -441,49 +473,67 @@
                 def _():
                     act(b_copy(t))
 
+    def keep(ref, value):
+        for c in range(2):
+            ref[c] = value[:, :, c * width : (c + 1) * width].reshape(bands * rows, width)
+
     @pl.when(is_reducer)
     def _():
         m_all = inbox_m.at[pl.ds(0, bands - 1)]
         pltpu.make_async_copy(m_all, m_all, m_recv).wait()
         left = inbox_m[...].astype(F32)
-        for c in range(2):
-            left_f[c] = left[:, :, c * width : (c + 1) * width].reshape(bands * rows, width)
         row_id = lax.broadcasted_iota(jnp.int32, (rows, 2 * width), 0) + number * rows
         lane_id = lax.broadcasted_iota(jnp.int32, (rows, 2 * width), 1)
         row_f = (row_id - (radius - 1)).astype(F32)
         lane_g = (jnp.where(lane_id >= width, lane_id - width, lane_id) - (radius - 1)).astype(F32)
         kin = (row_f * row_f + lane_g * lane_g) * (1.0 / float(radius * radius))
         right = left * kin[None]
+        keep(left_f, left)
+
+        def overlaps(source):
+            result = jnp.zeros((2 * bands, bands), F32)
+            for r in range(rows):
+                every = pl.ds(r, bands, stride=rows)
+                low = jnp.concatenate([left_f[0, every, :], left_f[1, every, :]], axis=1)
+                high_re, high_im = source[0, every, :], source[1, every, :]
+                stack = jnp.concatenate(
+                    [
+                        jnp.concatenate([high_re, high_im], axis=1),
+                        jnp.concatenate([-high_im, high_re], axis=1),
+                    ],
+                    axis=0,
+                )
+                result += dot_nt(stack.astype(BF16), low.astype(BF16))
+            return result * (1.0 / float(4 * radius * radius))
+
+        corr = overlaps(left_f)
         p_all = inbox_p.at[pl.ds(0, total - 1)]
         pltpu.make_async_copy(p_all, p_all, p_recv).wait()
         for g in range(groups):
             right += inbox_p[g * bands : (g + 1) * bands].astype(F32)
-        for c in range(2):
-            right_f[c] = right[:, :, c * width : (c + 1) * width].reshape(bands * rows, width)
-        result = jnp.zeros((bands, 4 * bands), F32)
-        for r in range(rows):
-            every = pl.ds(r, bands, stride=rows)
-            low_re, low_im = left_f[0, every, :], left_f[1, every, :]
-            high_re, high_im = right_f[0, every, :], right_f[1, every, :]
-            low = jnp.concatenate([low_re, low_im], axis=1)
-            stack = jnp.concatenate(
-                [
-                    jnp.concatenate([high_re, high_im], axis=1),
-                    jnp.concatenate([high_im, -high_re], axis=1),
-                    low,
-                    jnp.concatenate([low_im, -low_re], axis=1),
-                ],
-                axis=0,
-            )
-            result += dot_nt(low.astype(BF16), stack.astype(BF16))
-        result = result * (1.0 / float(4 * radius * radius))
-        fold = message.shape[1] // (4 * bands)
+        keep(right_f, right)
+        result = jnp.concatenate([overlaps(right_f), corr], axis=0)
         depth = message.shape[0]
         message[...] = jnp.concatenate(
-            [result[f * depth : (f + 1) * depth] for f in range(fold)], axis=1
+            [result[f : f + depth] for f in range(0, 4 * bands, depth)], axis=1
         )
         inbox_s[number] = message[...]
         b_each(lambda copy: copy.start())
+
+    for copy in x_copies:
+        copy.wait()
+    for k in range(1, groups):
+        mine += got[k - 1]
+    a_re = take_lanes(mine[:, :width], own_index)
+    a_im = take_lanes(mine[:, width:], own_index)
+    out_ref[0, 0] = jnp.where(present, kinetic * re + a_re, 0.0).astype(BF16)
+    out_ref[1, 0] = jnp.where(present, kinetic * im + a_im, 0.0).astype(BF16)
+
+    m_each(lambda copy: copy.wait_send(), False)
+    p_each(lambda copy: copy.wait_send(), False)
+
+    @pl.when(is_reducer)
+    def _():
         most = inbox_s.at[pl.ds(0, reducers - 1)]
         pltpu.make_async_copy(most, most, b_recv).wait()
 
@@ -494,16 +544,14 @@
     final = inbox_s[0]
     for r in range(1, reducers):
         final += inbox_s[r]
-    span = 4 * bands
-    fold = message.shape[1] // span
-    final = jnp.concatenate([final[:, f * span : (f + 1) * span] for f in range(fold)], axis=0)
-    red_ref[0] = final[:, :bands]
-    red_ref[1] = final[:, bands : 2 * bands]
-    corr_ref[0] = final[:, 2 * bands : 3 * bands]
-    corr_ref[1] = final[:, 3 * bands :]
-
-    m_each(lambda copy: copy.wait_send(), False)
-    p_each(lambda copy: copy.wait_send(), False)
+    final = jnp.concatenate(
+        [final[:, f : f + bands] for f in range(0, final.shape[1], bands)], axis=0
+    )
+    red_ref[0] = final[:bands]
+    red_ref[1] = final[bands : 2 * bands]
+    corr_ref[0] = final[2 * bands : 3 * bands]
+    corr_ref[1] = final[3 * bands :]
+
 
     @pl.when(is_reducer)
     def _():
@@ -533,9 +581,9 @@
     reducers = width // 16
     per_group = reducers // groups
     rows = width // reducers
-    fold = max(1, 128 // (4 * bands))
+    fold = max(1, 128 // bands)
     slot_lanes = -(-groups * slots // 128) * 128
-    tz, tx, ty, tr = tables(points, width, radius, groups, planes, plane_pad, coarse)
+    tz, tb, tx, ty, tr = tables(points, width, radius, groups, planes, plane_pad, coarse)
     vmem = pl.BlockSpec(memory_space=pltpu.VMEM)
     hbm = pl.BlockSpec(memory_space=pltpu.HBM)
     total = bands * groups
@@ -547,13 +595,14 @@
             pltpu.VMEM((2, bands, bands), F32),
             pltpu.VMEM((2, bands, bands), F32),
         ),
-        in_specs=[hbm] * 8,
+        in_specs=[hbm] * 9,
         out_specs=(vmem, vmem, vmem),
         scratch_shapes=[
             pltpu.VMEM(orbitals.shape, BF16),
             pltpu.VMEM(slot_sticks.shape, jnp.int32),
             pltpu.VMEM(stick_entries.shape, jnp.int32),
             pltpu.VMEM(tz.shape[1:], BF16),
+            pltpu.VMEM(tb.shape[1:], BF16),
             pltpu.VMEM(tx.shape, BF16),
             pltpu.VMEM(ty.shape, BF16),
             pltpu.VMEM(tr.shape, BF16),
@@ -562,7 +611,6 @@
             pltpu.VMEM((groups, slots, width), jnp.int32),
             pltpu.VMEM((groups - 1, 2, slots, width), BF16),
             pltpu.VMEM((groups, slots, 2 * width), BF16),
-            pltpu.VMEM((2, 2 * width, plane_pad), BF16),
             pltpu.VMEM((groups - 1, slots, 2 * width), F32),
             pltpu.VMEM((groups - 1, slots, 2 * width), F32),
             pltpu.VMEM((width, 2 * width), BF16),
@@ -571,10 +619,11 @@
             pltpu.VMEM((total, rows, 2 * width), BF16),
             pltpu.VMEM((2, bands * rows, width), F32),
             pltpu.VMEM((2, bands * rows, width), F32),
-            pltpu.VMEM((bands // fold, 4 * bands * fold), F32),
-            pltpu.VMEM((reducers, bands // fold, 4 * bands * fold), F32),
-            dma((8,)),
+            pltpu.VMEM((4 * bands // fold, bands * fold), F32),
+            pltpu.VMEM((reducers, 4 * bands // fold, bands * fold), F32),
+            dma((9,)),
             pltpu.SemaphoreType.REGULAR((2,)),
+            pltpu.SemaphoreType.REGULAR,
             dma((groups - 1,)),
             dma((groups - 1,)),
             dma((groups - 1,)),
@@ -589,7 +638,7 @@
         compiler_params=pltpu.CompilerParams(
             collective_id=0, has_side_effects=True, vmem_limit_bytes=60000000
         ),
-    )(orbitals, slot_sticks, stick_entries, potential, tz, tx, ty, tr)
+    )(orbitals, slot_sticks, stick_entries, potential, tz, tb, tx, ty, tr)
     return pl.pallas_call(
         write_out,
         out_shape=[jax.ShapeDtypeStruct(r.shape, r.dtype) for r in results],

time: 20.4 us -> 19.7 us (0.966)
  Pallas kernels: 19.6 us -> 18.9 us
    pallas_call x1, Pallas kernels: 19 us -> 18.3 us  [body(): pl.pallas_call(functools.partial(kernel, bands, groups, points, radius),...]
where the time goes in v3:
time: 19.7 us; the launch traced here: 19.6 us
  Pallas kernels  18.9 us (96%)
  between operations  0.64 us (3%)
    pallas_call x1, Pallas kernels, body(): pl.pallas_call(functools.partial(kernel, bands, groups, points, radius),...  18.3 us
    pallas_call x1, Pallas kernels, body(): pl.pallas_call(write_out, out_shape=[jax.ShapeDtypeStruct(r.shape, r.dtyp...  0.65 us

profile of v3, /device:TPU:0, one launch (start us, length us, event | category | flops | bytes accessed | tf_op | source)
XLA Modules:
  0.0 19.6 jit_solution(9825862541556710970)
XLA Ops:
  0.6 18.3 %shard_map.112 = (bf16[2,1,80,128]{3,2,1,0:T(8,128)(2,1)S(1)}, f32[2,16,16]{2,1,0:T(8,128)S(1)}, f32[2,16,16]{2,1,0:T(8,128)S(1)}) custom-call(bf16[2,1,80,128]{3,2,1,0:T(8,128)(2,1)} %orb_hbm.1, s32[160]{0:T(256)} %slots_hbm.1, s32[160,128]{1,0:T(8,128)} %entries_hbm.1, f32[240,480]{1,0:T(8,128)} %pot_hbm.1, bf16[2,512,512]{2,1,0:T(8,128)(2,1)} %constant.10.clone.tz_hbm, ...), custom_call_target="tpu_custom_call" | custom-call | tf_op jit(solution)/shard_map/pallas_call | solution.py:591
  18.9 0.7 %shard_map.113 = (bf16[2,1,80,128]{3,2,1,0:T(8,128)(2,1)}, f32[2,16,16]{2,1,0:T(8,128)}, f32[2,16,16]{2,1,0:T(8,128)}) custom-call(bf16[2,1,80,128]{3,2,1,0:T(8,128)(2,1)S(1)} %get-tuple-element.6.out_ref, f32[2,16,16]{2,1,0:T(8,128)S(1)} %get-tuple-element.7.corr_ref, f32[2,16,16]{2,1,0:T(8,128)S(1)} %get-tuple-element.8.red_ref), custom_call_target="tpu_custom_call" | custom-call | tf_op jit(solution)/shard_map/pallas_call | solution.py:642

commit v4 on v3

--- a/solution.py
+++ b/solution.py
@@ -21,11 +21,6 @@
     high = table.astype(np.float32).astype(BF16)
     low = (table - high.astype(np.float64)).astype(np.float32).astype(BF16)
     return np.stack([high, low])
-
-
-def triple(pair, axis):
-    high, low = (np.take(pair, i, axis=pair.ndim - 3) for i in range(2))
-    return np.concatenate([high, high, low], axis=axis)
 
 
 def tables(points, width, radius, groups, planes, plane_pad, coarse):
@@ -54,10 +49,10 @@
     resample /= points
     z_tabs = np.stack(z_tabs)
     return (
-        z_tabs.reshape(groups, 2 * z_tabs.shape[2], z_tabs.shape[3]),
-        triple(np.swapaxes(z_tabs, 2, 3), 1),
-        triple(split_np(forward), 1),
-        triple(split_np(forward.T.copy()), 1),
+        z_tabs,
+        np.swapaxes(z_tabs, 2, 3).copy(),
+        split_np(forward),
+        split_np(forward.T.copy()),
         split_np(resample),
     )
 
@@ -142,12 +137,13 @@
     band = lax.axis_index("band")
     ga = lax.axis_index("ga")
     total = bands * groups
-    me = ga * bands + band
+    twin = band + 1 - 2 * lax.rem(band, 2)
+    me = ga * bands + twin
     slots = orb_hbm.shape[2]
     width = orb_hbm.shape[3]
     planes = pot_hbm.shape[0]
     plane_pad = pot.shape[0]
-    coarse = tx.shape[0] // 2
+    coarse = tx.shape[1] // 2
     reducers = inbox_s.shape[0]
     rows = width // reducers
     per_group = reducers // groups
@@ -174,15 +170,16 @@
     has_low = band >= block
     has_high = band < bands - block
     barrier = pltpu.get_barrier_semaphore()
-    for c in range(block):
-        for g in range(groups):
-            if g or c:
-                pl.semaphore_signal(
-                    barrier,
-                    inc=1,
-                    device_id=(base + lax.rem(place + c, block), lax.rem(ga + g, groups)),
-                    device_id_type=MESH,
-                )
+    across = band + 2 - 4 * lax.rem(lax.div(band, 2), 2)
+
+    def greet(to_band, to_ga, semaphore=barrier):
+        pl.semaphore_signal(semaphore, inc=1, device_id=(to_band, to_ga), device_id_type=MESH)
+
+    for k in range(1, groups):
+        greet(twin, lax.rem(ga + k, groups))
+        greet(band, lax.rem(ga + k, groups))
+    greet(twin, ga)
+    greet(across, ga)
 
     def near(semaphore_low, semaphore_high):
         @pl.when(has_low)
@@ -217,21 +214,25 @@
 
     load_orb.wait()
     pl.semaphore_wait(
-        barrier, block * groups - 1 + has_low.astype(jnp.int32) + has_high.astype(jnp.int32)
+        barrier, 2 * groups + has_low.astype(jnp.int32) + has_high.astype(jnp.int32)
     )
     s_copies = []
-    for k in range(1, groups):
+    for k in range(1, groups + 1):
         copy = pltpu.make_async_remote_copy(
             src_ref=orb_ref.at[:, 0],
-            dst_ref=raw.at[k - 1],
+            dst_ref=raw.at[ga],
             send_sem=s_send.at[k - 1],
-            recv_sem=s_recv.at[k - 1],
-            device_id=(band, lax.rem(ga + k, groups)),
+            recv_sem=s_recv.at[ga],
+            device_id=(twin, lax.rem(ga + k, groups)),
             device_id_type=MESH,
         )
         copy.start()
         s_copies.append(copy)
-    near(near_sem.at[0], near_sem.at[1])
+
+    def arrived(ref, sem, g):
+        pltpu.make_async_copy(ref.at[g], ref.at[g], sem.at[g]).wait()
+
+    greet(across, ga, near_sem.at[2])
 
     load_entries.wait()
     load_slots.wait()
@@ -259,7 +260,10 @@
     for g in range(groups):
         inv_ref[g] = found[g * slots : (g + 1) * slots]
 
-    def spread_of(g, re, im):
+    def spread_of(g):
+        arrived(raw, s_recv, g)
+        re = raw[g, 0].astype(F32)
+        im = raw[g, 1].astype(F32)
         inverse = inv_ref[g]
         filled = inverse >= 0
         index = jnp.maximum(inverse, 0)
@@ -268,23 +272,25 @@
 
     re = orb_ref[0, 0].astype(F32)
     im = orb_ref[1, 0].astype(F32)
-    spread_of(ga, re, im)
-
-    near_wait()
+    spread_of(ga)
+
     rounds = max(blocks // 2, 1)
-    if rounds > 1:
-        near(near_sem.at[0], near_sem.at[1])
+    pl.semaphore_wait(near_sem.at[2], 1)
+    near(near_sem.at[0], near_sem.at[1])
 
     load_pot.wait()
     load_tr.wait()
     pot_hi, pot_lo = split(pot[...])
     weight = dot_nt(tr[0], pot_hi) + dot_nt(tr[0], pot_lo) + dot_nt(tr[1], pot_hi)
 
-    for k, copy in enumerate(s_copies, 1):
-        copy.wait()
-        spread_of(
-            lax.rem(ga - k + groups, groups), raw[k - 1, 0].astype(F32), raw[k - 1, 1].astype(F32)
-        )
+    near_wait()
+    if rounds > 1:
+        near(near_sem.at[0], near_sem.at[1])
+
+    for k in range(1, groups):
+        spread_of(lax.rem(ga + k, groups))
+    for copy in s_copies:
+        copy.wait_send()
     all_sticks = slots_ref[...].reshape(1, all_slots)
     sticks = [all_sticks[:, g * slots : (g + 1) * slots] for g in range(groups)]
     dense = jnp.zeros((width, 2 * width), F32)
@@ -303,51 +309,45 @@
     def place_of(r):
         return first_band + 2 * lax.rem(r, per_group), lax.div(r, per_group)
 
-    def m_copy(q):
+    def other(to_band, to_ga):
+        own = (to_band == band) & (to_ga == ga)
+        return jnp.where(own, band - 1, to_band), to_ga
+
+    m_copies = []
+    for q in range(per_group):
         start = pl.multiple_of((ga * per_group + q) * rows, rows)
-        return pltpu.make_async_remote_copy(
-            src_ref=dense_ref.at[pl.ds(start, rows)],
-            dst_ref=inbox_m.at[band],
-            send_sem=m_send.at[q],
-            recv_sem=m_recv,
-            device_id=(first_band + 2 * q, ga),
-            device_id_type=MESH,
+        m_copies.append(
+            pltpu.make_async_remote_copy(
+                src_ref=dense_ref.at[pl.ds(start, rows)],
+                dst_ref=inbox_m.at[twin],
+                send_sem=m_send.at[q],
+                recv_sem=m_recv,
+                device_id=other(first_band + 2 * q, ga),
+                device_id_type=MESH,
+            )
         )
-
-    def m_each(act, own):
-        for q in range(per_group):
-            mine = band == first_band + 2 * q
-
-            @pl.when(jnp.logical_not(mine))
-            def _(q=q):
-                act(m_copy(q))
-
-            if own:
-
-                @pl.when(mine)
-                def _(q=q):
-                    start = pl.multiple_of((ga * per_group + q) * rows, rows)
-                    inbox_m[band] = dense_ref[pl.ds(start, rows), :]
-
-    m_each(lambda copy: copy.start(), True)
+        m_copies[-1].start()
 
     load_tz.wait()
     pair = jnp.concatenate([dense, dense], axis=1)
-    columns = [dot(pair, tz[:, :plane_pad]), dot(pair, tz[:, plane_pad:])]
+    z_table = jnp.concatenate([tz[0], tz[1]], axis=0)
+    columns = [dot(pair, z_table[:, :plane_pad]), dot(pair, z_table[:, plane_pad:])]
     columns = jnp.concatenate(columns, axis=0)
     load_tx.wait()
+    x_table = jnp.concatenate([tx[0], tx[0], tx[1]], axis=1)
     columns = thirds(columns, 0)
     quarter = coarse // 2
     field = jnp.concatenate(
-        [dot(tx[i * quarter : (i + 1) * quarter], columns) for i in range(4)], axis=0
+        [dot(x_table[i * quarter : (i + 1) * quarter], columns) for i in range(4)], axis=0
     )
     product = jnp.concatenate([field[:coarse] * weight, field[coarse:] * weight], axis=0)
     product = thirds(product, 0)
     load_ty.wait()
-    back = jnp.concatenate([dot(ty[:width], product), dot(ty[width:], product)], axis=0)
+    y_table = jnp.concatenate([ty[0], ty[0], ty[1]], axis=1)
+    back = jnp.concatenate([dot(y_table[:width], product), dot(y_table[width:], product)], axis=0)
     back = thirds(jnp.concatenate([back[:width], back[width:]], axis=1), 1)
     load_tb.wait()
-    spectra = dot(back, tb[...])
+    spectra = dot(back, jnp.concatenate([tb[0], tb[0], tb[1]], axis=0))
     spectra = spectra * (1.0 / float(points * coarse))
     spec_hi, spec_lo = split(spectra)
     pdense[...] = spec_hi
@@ -366,33 +366,20 @@
             bit *= 2
         return g * per_group + q
 
-    def p_copy(r):
-        return pltpu.make_async_remote_copy(
-            src_ref=pdense.at[pl.ds(pl.multiple_of(r * rows, rows), rows)],
-            dst_ref=inbox_p.at[me],
-            send_sem=p_send.at[r],
-            recv_sem=p_recv,
-            device_id=place_of(r),
-            device_id_type=MESH,
+    p_copies = []
+    for far in reversed(range(reducers)):
+        r = far_reducer(far)
+        p_copies.append(
+            pltpu.make_async_remote_copy(
+                src_ref=pdense.at[pl.ds(pl.multiple_of(r * rows, rows), rows)],
+                dst_ref=inbox_p.at[me],
+                send_sem=p_send.at[far],
+                recv_sem=p_recv,
+                device_id=other(*place_of(r)),
+                device_id_type=MESH,
+            )
         )
-
-    def p_each(act, own):
-        for far in reversed(range(reducers)):
-            r = far_reducer(far)
-            to_band, to_ga = place_of(r)
-            mine = me == to_ga * bands + to_band
-
-            @pl.when(jnp.logical_not(mine))
-            def _(r=r):
-                act(p_copy(r))
-
-            if own:
-
-                @pl.when(mine)
-                def _(r=r):
-                    inbox_p[me] = pdense[pl.ds(pl.multiple_of(r * rows, rows), rows), :]
-
-    p_each(lambda copy: copy.start(), True)
+        p_copies[-1].start()
 
     @pl.when(lax.rem(band, 2) == 0)
     def _():
@@ -417,17 +404,17 @@
         stick = stick_column(target)
         choose = jnp.where(stick == lane_f, 1.0, 0.0).astype(BF16)
         mine = dot(choose, spec_hi) + dot(choose, spec_lo)
-        if k < groups:
-            part[k - 1] = mine
-            copy = pltpu.make_async_remote_copy(
+        part[k - 1] = mine
+        x_copies.append(
+            pltpu.make_async_remote_copy(
                 src_ref=part.at[k - 1],
-                dst_ref=got.at[k - 1],
+                dst_ref=got.at[ga],
                 send_sem=x_send.at[k - 1],
-                recv_sem=x_recv.at[k - 1],
-                device_id=(band, target),
+                recv_sem=x_recv.at[ga],
+                device_id=(twin, target),
                 device_id_type=MESH,
             )
-            x_copies.append(copy)
+        )
 
     own = entries_ref[pl.ds(pl.multiple_of(ga * slots, 8), slots)]
     present = own >= 0
@@ -447,18 +434,23 @@
     is_reducer = (offset >= 0) & (offset < 2 * per_group) & (lax.rem(band + 1, 2) == 0)
     number = ga * per_group + lax.div(jnp.clip(offset, 0, 2 * per_group - 1), 2)
 
+    order = band * groups + ga
+
     def b_copy(t):
+        if isinstance(t, int):
+            to_band, to_ga = t // groups, t % groups
+        else:
+            to_band, to_ga = lax.div(t, groups), lax.rem(t, groups)
         return pltpu.make_async_remote_copy(
             src_ref=message,
             dst_ref=inbox_s.at[number],
             send_sem=b_send.at[t],
             recv_sem=b_recv,
-            device_id=(t // groups, t % groups) if isinstance(t, int) else (lax.div(t, groups), lax.rem(t, groups)),
+            device_id=(to_band, to_ga),
             device_id_type=MESH,
         )
 
     def b_each(act):
-        order = band * groups + ga
         if total <= 64:
             for t in range(total):
 
@@ -481,6 +473,9 @@
     def _():
         m_all = inbox_m.at[pl.ds(0, bands - 1)]
         pltpu.make_async_copy(m_all, m_all, m_recv).wait()
+        own_rows = pl.ds(pl.multiple_of(number * rows, rows), rows)
+        inbox_m[twin] = dense_ref[own_rows, :]
+        inbox_p[me] = pdense[own_rows, :]
         left = inbox_m[...].astype(F32)
         row_id = lax.broadcasted_iota(jnp.int32, (rows, 2 * width), 0) + number * rows
         lane_id = lax.broadcasted_iota(jnp.int32, (rows, 2 * width), 1)
@@ -520,22 +515,30 @@
         inbox_s[number] = message[...]
         b_each(lambda copy: copy.start())
 
-    for copy in x_copies:
-        copy.wait()
-    for k in range(1, groups):
-        mine += got[k - 1]
+    for g in range(groups):
+        arrived(got, x_recv, g)
+    mine = got[0]
+    for g in range(1, groups):
+        mine += got[g]
     a_re = take_lanes(mine[:, :width], own_index)
     a_im = take_lanes(mine[:, width:], own_index)
     out_ref[0, 0] = jnp.where(present, kinetic * re + a_re, 0.0).astype(BF16)
     out_ref[1, 0] = jnp.where(present, kinetic * im + a_im, 0.0).astype(BF16)
 
-    m_each(lambda copy: copy.wait_send(), False)
-    p_each(lambda copy: copy.wait_send(), False)
+    for copy in m_copies + p_copies + x_copies:
+        copy.wait_send()
 
     @pl.when(is_reducer)
     def _():
         most = inbox_s.at[pl.ds(0, reducers - 1)]
         pltpu.make_async_copy(most, most, b_recv).wait()
+
+    beside = (offset + 1 >= 0) & (offset + 1 < 2 * per_group) & (lax.rem(band, 2) == 0)
+
+    @pl.when(beside)
+    def _():
+        pltpu.make_async_copy(inbox_m.at[0], inbox_m.at[0], m_recv).wait()
+        pltpu.make_async_copy(inbox_p.at[0], inbox_p.at[0], p_recv).wait()
 
     @pl.when(jnp.logical_not(is_reducer))
     def _():
@@ -609,10 +612,10 @@
             pltpu.VMEM((plane_pad, points), F32),
             pltpu.VMEM((width, slot_lanes), F32),
             pltpu.VMEM((groups, slots, width), jnp.int32),
-            pltpu.VMEM((groups - 1, 2, slots, width), BF16),
+            pltpu.VMEM((groups, 2, slots, width), BF16),
             pltpu.VMEM((groups, slots, 2 * width), BF16),
-            pltpu.VMEM((groups - 1, slots, 2 * width), F32),
-            pltpu.VMEM((groups - 1, slots, 2 * width), F32),
+            pltpu.VMEM((groups, slots, 2 * width), F32),
+            pltpu.VMEM((groups, slots, 2 * width), F32),
             pltpu.VMEM((width, 2 * width), BF16),
             pltpu.VMEM((width, 2 * width), BF16),
             pltpu.VMEM((bands, rows, 2 * width), BF16),
@@ -622,12 +625,12 @@
             pltpu.VMEM((4 * bands // fold, bands * fold), F32),
             pltpu.VMEM((reducers, 4 * bands // fold, bands * fold), F32),
             dma((9,)),
-            pltpu.SemaphoreType.REGULAR((2,)),
+            pltpu.SemaphoreType.REGULAR((3,)),
             pltpu.SemaphoreType.REGULAR,
-            dma((groups - 1,)),
-            dma((groups - 1,)),
-            dma((groups - 1,)),
-            dma((groups - 1,)),
+            dma((groups,)),
+            dma((groups,)),
+            dma((groups,)),
+            dma((groups,)),
             dma((per_group,)),
             dma,
             dma((reducers,)),

time: 19.7 us -> 19.3 us (0.980)
  Pallas kernels: 18.9 us -> 18.5 us
    pallas_call x1, Pallas kernels: 18.3 us -> 17.8 us  [body(): pl.pallas_call(functools.partial(kernel, bands, groups, points, radius),...]
where the time goes in v4:
time: 19.3 us; the launch traced here: 19.1 us
  Pallas kernels  18.5 us (96%)
  between operations  0.64 us (3%)
    pallas_call x1, Pallas kernels, body(): pl.pallas_call(functools.partial(kernel, bands, groups, points, radius),...  17.8 us
    pallas_call x1, Pallas kernels, body(): pl.pallas_call(write_out, out_shape=[jax.ShapeDtypeStruct(r.shape, r.dtyp...  0.65 us

profile of v4, /device:TPU:0, one launch (start us, length us, event | category | flops | bytes accessed | tf_op | source)
XLA Modules:
  0.0 19.1 jit_solution(7380545610529168533)
XLA Ops:
  0.6 17.8 %shard_map.112 = (bf16[2,1,80,128]{3,2,1,0:T(8,128)(2,1)S(1)}, f32[2,16,16]{2,1,0:T(8,128)S(1)}, f32[2,16,16]{2,1,0:T(8,128)S(1)}) custom-call(bf16[2,1,80,128]{3,2,1,0:T(8,128)(2,1)} %orb_hbm.1, s32[160]{0:T(256)} %slots_hbm.1, s32[160,128]{1,0:T(8,128)} %entries_hbm.1, f32[240,480]{1,0:T(8,128)} %pot_hbm.1, ...), custom_call_target="tpu_custom_call" | custom-call | tf_op jit(solution)/shard_map/pallas_call | solution.py:594
  18.5 0.7 %shard_map.113 = (bf16[2,1,80,128]{3,2,1,0:T(8,128)(2,1)}, f32[2,16,16]{2,1,0:T(8,128)}, f32[2,16,16]{2,1,0:T(8,128)}) custom-call(bf16[2,1,80,128]{3,2,1,0:T(8,128)(2,1)S(1)} %get-tuple-element.6.out_ref, f32[2,16,16]{2,1,0:T(8,128)S(1)} %get-tuple-element.7.corr_ref, f32[2,16,16]{2,1,0:T(8,128)S(1)} %get-tuple-element.8.red_ref), custom_call_target="tpu_custom_call" | custom-call | tf_op jit(solution)/shard_map/pallas_call | solution.py:645

commit v5 on v4

--- a/solution.py
+++ b/solution.py
@@ -122,7 +122,6 @@
     inbox_s,
     load_sem,
     near_sem,
-    pair_sem,
     s_send,
     s_recv,
     x_send,
@@ -301,6 +300,20 @@
     dense = dense.astype(BF16)
     dense_ref[...] = dense
 
+    load_tz.wait()
+    pair = jnp.concatenate([dense, dense], axis=1)
+    z_table = jnp.concatenate([tz[0], tz[1]], axis=0)
+    columns = [dot(pair, z_table[:, :plane_pad]), dot(pair, z_table[:, plane_pad:])]
+    columns = jnp.concatenate(columns, axis=0)
+    load_tx.wait()
+    x_table = jnp.concatenate([tx[0], tx[0], tx[1]], axis=1)
+    columns = thirds(columns, 0)
+    quarter = coarse // 2
+    field = jnp.concatenate(
+        [dot(x_table[i * quarter : (i + 1) * quarter], columns) for i in range(4)], axis=0
+    )
+    product = jnp.concatenate([field[:coarse] * weight, field[coarse:] * weight], axis=0)
+    product = thirds(product, 0)
     for r in range(1, rounds):
         near_wait()
         if r < rounds - 1:
@@ -328,20 +341,6 @@
         )
         m_copies[-1].start()
 
-    load_tz.wait()
-    pair = jnp.concatenate([dense, dense], axis=1)
-    z_table = jnp.concatenate([tz[0], tz[1]], axis=0)
-    columns = [dot(pair, z_table[:, :plane_pad]), dot(pair, z_table[:, plane_pad:])]
-    columns = jnp.concatenate(columns, axis=0)
-    load_tx.wait()
-    x_table = jnp.concatenate([tx[0], tx[0], tx[1]], axis=1)
-    columns = thirds(columns, 0)
-    quarter = coarse // 2
-    field = jnp.concatenate(
-        [dot(x_table[i * quarter : (i + 1) * quarter], columns) for i in range(4)], axis=0
-    )
-    product = jnp.concatenate([field[:coarse] * weight, field[coarse:] * weight], axis=0)
-    product = thirds(product, 0)
     load_ty.wait()
     y_table = jnp.concatenate([ty[0], ty[0], ty[1]], axis=1)
     back = jnp.concatenate([dot(y_table[:width], product), dot(y_table[width:], product)], axis=0)
@@ -380,10 +379,6 @@
             )
         )
         p_copies[-1].start()
-
-    @pl.when(lax.rem(band, 2) == 0)
-    def _():
-        pl.semaphore_signal(pair_sem, inc=1, device_id=(band + 1, ga), device_id_type=MESH)
 
     eye = lax.broadcasted_iota(jnp.int32, (slots, slots), 0) == lax.broadcasted_iota(
         jnp.int32, (slots, slots), 1
@@ -422,10 +417,6 @@
     gz = (own - (radius - 1)).astype(F32)
     kinetic = (gx * gx + gz * gz) * (1.0 / float(radius * radius))
     own_index = jnp.maximum(own, 0)
-
-    @pl.when(lax.rem(band, 2) == 1)
-    def _():
-        pl.semaphore_wait(pair_sem, 1)
 
     for copy in x_copies:
         copy.start()
@@ -626,7 +617,6 @@
             pltpu.VMEM((reducers, 4 * bands // fold, bands * fold), F32),
             dma((9,)),
             pltpu.SemaphoreType.REGULAR((3,)),
-            pltpu.SemaphoreType.REGULAR,
             dma((groups,)),
             dma((groups,)),
             dma((groups,)),

time: 19.3 us -> 19 us (0.984)
  Pallas kernels: 18.5 us -> 18.2 us
    pallas_call x1, Pallas kernels: 17.8 us -> 17.6 us  [body(): pl.pallas_call(functools.partial(kernel, bands, groups, points, radius),...]
where the time goes in v5:
time: 19 us; the launch traced here: 18.9 us
  Pallas kernels  18.2 us (96%)
  between operations  0.64 us (3%)
    pallas_call x1, Pallas kernels, body(): pl.pallas_call(functools.partial(kernel, bands, groups, points, radius),...  17.6 us
    pallas_call x1, Pallas kernels, body(): pl.pallas_call(write_out, out_shape=[jax.ShapeDtypeStruct(r.shape, r.dtyp...  0.65 us

profile of v5, /device:TPU:0, one launch (start us, length us, event | category | flops | bytes accessed | tf_op | source)
XLA Modules:
  0.0 18.9 jit_solution(14220534756502860151)
XLA Ops:
  0.6 17.6 %shard_map.112 = (bf16[2,1,80,128]{3,2,1,0:T(8,128)(2,1)S(1)}, f32[2,16,16]{2,1,0:T(8,128)S(1)}, f32[2,16,16]{2,1,0:T(8,128)S(1)}) custom-call(bf16[2,1,80,128]{3,2,1,0:T(8,128)(2,1)} %orb_hbm.1, s32[160]{0:T(256)} %slots_hbm.1, s32[160,128]{1,0:T(8,128)} %entries_hbm.1, f32[240,480]{1,0:T(8,128)} %pot_hbm.1, ...), custom_call_target="tpu_custom_call" | custom-call | tf_op jit(solution)/shard_map/pallas_call | solution.py:585
  18.2 0.7 %shard_map.113 = (bf16[2,1,80,128]{3,2,1,0:T(8,128)(2,1)}, f32[2,16,16]{2,1,0:T(8,128)}, f32[2,16,16]{2,1,0:T(8,128)}) custom-call(bf16[2,1,80,128]{3,2,1,0:T(8,128)(2,1)S(1)} %get-tuple-element.6.out_ref, f32[2,16,16]{2,1,0:T(8,128)S(1)} %get-tuple-element.7.corr_ref, f32[2,16,16]{2,1,0:T(8,128)S(1)} %get-tuple-element.8.red_ref), custom_call_target="tpu_custom_call" | custom-call | tf_op jit(solution)/shard_map/pallas_call | solution.py:635

commit v6 on v5

--- a/solution.py
+++ b/solution.py
@@ -286,17 +286,25 @@
     if rounds > 1:
         near(near_sem.at[0], near_sem.at[1])
 
+    all_sticks = slots_ref[...].reshape(1, all_slots)
+    sticks = [all_sticks[:, g * slots : (g + 1) * slots] for g in range(groups)]
+    sub = lax.broadcasted_iota(jnp.int32, (width, slots), 0)
+
+    def chosen_of(g):
+        row = sticks[0]
+        for other_ga in range(1, groups):
+            row = jnp.where(g == other_ga, sticks[other_ga], row)
+        return jnp.where(sub == row, 1.0, 0.0).astype(BF16)
+
+    chosen = [chosen_of(lax.rem(ga + k, groups)) for k in range(1, groups)]
+    dense = dot(chosen_of(ga), spread[ga])
+
     for k in range(1, groups):
         spread_of(lax.rem(ga + k, groups))
     for copy in s_copies:
         copy.wait_send()
-    all_sticks = slots_ref[...].reshape(1, all_slots)
-    sticks = [all_sticks[:, g * slots : (g + 1) * slots] for g in range(groups)]
-    dense = jnp.zeros((width, 2 * width), F32)
-    sub = lax.broadcasted_iota(jnp.int32, (width, slots), 0)
-    for g in range(groups):
-        choose = jnp.where(sub == sticks[g], 1.0, 0.0).astype(BF16)
-        dense += dot(choose, spread[g])
+    for k in range(1, groups):
+        dense += dot(chosen[k - 1], spread[lax.rem(ga + k, groups)])
     dense = dense.astype(BF16)
     dense_ref[...] = dense
 

time: 19 us -> 19 us (level)
  no operation moved by 1% of the time
where the time goes in v6:
time: 19 us; the launch traced here: 18.9 us
  Pallas kernels  18.2 us (96%)
  between operations  0.64 us (3%)
    pallas_call x1, Pallas kernels, body(): pl.pallas_call(functools.partial(kernel, bands, groups, points, radius),...  17.6 us
    pallas_call x1, Pallas kernels, body(): pl.pallas_call(write_out, out_shape=[jax.ShapeDtypeStruct(r.shape, r.dtyp...  0.65 us

profile of v6, /device:TPU:0, one launch (start us, length us, event | category | flops | bytes accessed | tf_op | source)
XLA Modules:
  0.0 18.9 jit_solution(4060985925157177915)
XLA Ops:
  0.6 17.6 %shard_map.112 = (bf16[2,1,80,128]{3,2,1,0:T(8,128)(2,1)S(1)}, f32[2,16,16]{2,1,0:T(8,128)S(1)}, f32[2,16,16]{2,1,0:T(8,128)S(1)}) custom-call(bf16[2,1,80,128]{3,2,1,0:T(8,128)(2,1)} %orb_hbm.1, s32[160]{0:T(256)} %slots_hbm.1, s32[160,128]{1,0:T(8,128)} %entries_hbm.1, f32[240,480]{1,0:T(8,128)} %pot_hbm.1, ...), custom_call_target="tpu_custom_call" | custom-call | tf_op jit(solution)/shard_map/pallas_call | solution.py:593
  18.2 0.7 %shard_map.113 = (bf16[2,1,80,128]{3,2,1,0:T(8,128)(2,1)}, f32[2,16,16]{2,1,0:T(8,128)}, f32[2,16,16]{2,1,0:T(8,128)}) custom-call(bf16[2,1,80,128]{3,2,1,0:T(8,128)(2,1)S(1)} %get-tuple-element.6.out_ref, f32[2,16,16]{2,1,0:T(8,128)S(1)} %get-tuple-element.7.corr_ref, f32[2,16,16]{2,1,0:T(8,128)S(1)} %get-tuple-element.8.red_ref), custom_call_target="tpu_custom_call" | custom-call | tf_op jit(solution)/shard_map/pallas_call | solution.py:643

commit v7 on v6

--- a/solution.py
+++ b/solution.py
@@ -217,16 +217,17 @@
     )
     s_copies = []
     for k in range(1, groups + 1):
-        copy = pltpu.make_async_remote_copy(
-            src_ref=orb_ref.at[:, 0],
-            dst_ref=raw.at[ga],
-            send_sem=s_send.at[k - 1],
-            recv_sem=s_recv.at[ga],
-            device_id=(twin, lax.rem(ga + k, groups)),
-            device_id_type=MESH,
-        )
-        copy.start()
-        s_copies.append(copy)
+        for c in range(2):
+            copy = pltpu.make_async_remote_copy(
+                src_ref=orb_ref.at[c, 0],
+                dst_ref=raw.at[ga, c],
+                send_sem=s_send.at[k - 1, c],
+                recv_sem=s_recv.at[ga, c],
+                device_id=(twin, lax.rem(ga + k, groups)),
+                device_id_type=MESH,
+            )
+            copy.start()
+            s_copies.append(copy)
 
     def arrived(ref, sem, g):
         pltpu.make_async_copy(ref.at[g], ref.at[g], sem.at[g]).wait()
@@ -260,14 +261,13 @@
         inv_ref[g] = found[g * slots : (g + 1) * slots]
 
     def spread_of(g):
-        arrived(raw, s_recv, g)
-        re = raw[g, 0].astype(F32)
-        im = raw[g, 1].astype(F32)
         inverse = inv_ref[g]
         filled = inverse >= 0
         index = jnp.maximum(inverse, 0)
-        spread[g, :, :width] = jnp.where(filled, take_lanes(re, index), 0.0).astype(BF16)
-        spread[g, :, width:] = jnp.where(filled, take_lanes(im, index), 0.0).astype(BF16)
+        for c in range(2):
+            pltpu.make_async_copy(raw.at[g, c], raw.at[g, c], s_recv.at[g, c]).wait()
+            value = take_lanes(raw[g, c].astype(F32), index)
+            spread[g, :, c * width : (c + 1) * width] = jnp.where(filled, value, 0.0).astype(BF16)
 
     re = orb_ref[0, 0].astype(F32)
     im = orb_ref[1, 0].astype(F32)
@@ -625,8 +625,8 @@
             pltpu.VMEM((reducers, 4 * bands // fold, bands * fold), F32),
             dma((9,)),
             pltpu.SemaphoreType.REGULAR((3,)),
-            dma((groups,)),
-            dma((groups,)),
+            dma((groups, 2)),
+            dma((groups, 2)),
             dma((groups,)),
             dma((groups,)),
             dma((per_group,)),

time: 19 us -> 19.1 us (level)
  no operation moved by 1% of the time
where the time goes in v7:
time: 19.1 us; the launch traced here: 18.9 us
  Pallas kernels  18.3 us (96%)
  between operations  0.64 us (3%)
    pallas_call x1, Pallas kernels, body(): pl.pallas_call(functools.partial(kernel, bands, groups, points, radius),...  17.6 us
    pallas_call x1, Pallas kernels, body(): pl.pallas_call(write_out, out_shape=[jax.ShapeDtypeStruct(r.shape, r.dtyp...  0.65 us

profile of v7, /device:TPU:0, one launch (start us, length us, event | category | flops | bytes accessed | tf_op | source)
XLA Modules:
  0.0 18.9 jit_solution(3718202688136644959)
XLA Ops:
  0.6 17.6 %shard_map.112 = (bf16[2,1,80,128]{3,2,1,0:T(8,128)(2,1)S(1)}, f32[2,16,16]{2,1,0:T(8,128)S(1)}, f32[2,16,16]{2,1,0:T(8,128)S(1)}) custom-call(bf16[2,1,80,128]{3,2,1,0:T(8,128)(2,1)} %orb_hbm.1, s32[160]{0:T(256)} %slots_hbm.1, s32[160,128]{1,0:T(8,128)} %entries_hbm.1, f32[240,480]{1,0:T(8,128)} %pot_hbm.1, ...), custom_call_target="tpu_custom_call" | custom-call | tf_op jit(solution)/shard_map/pallas_call | solution.py:593
  18.3 0.7 %shard_map.113 = (bf16[2,1,80,128]{3,2,1,0:T(8,128)(2,1)}, f32[2,16,16]{2,1,0:T(8,128)}, f32[2,16,16]{2,1,0:T(8,128)}) custom-call(bf16[2,1,80,128]{3,2,1,0:T(8,128)(2,1)S(1)} %get-tuple-element.6.out_ref, f32[2,16,16]{2,1,0:T(8,128)S(1)} %get-tuple-element.7.corr_ref, f32[2,16,16]{2,1,0:T(8,128)S(1)} %get-tuple-element.8.red_ref), custom_call_target="tpu_custom_call" | custom-call | tf_op jit(solution)/shard_map/pallas_call | solution.py:643
